TPU v7x, 32 devices: a whole 2x2x4 slice. The times are simulated.
32 devices in a mesh: dp: 4 (over x, y), tp: 8 (over z, core).
Axes of the slice: x: 2, y: 2, z: 4, core: 2. Of those that a mesh axis runs over, the one named last changes fastest.
Arguments:
- residual: float32 [1024, 2048], P('dp'), parts along dimension 0
- norm_w: bfloat16 [2, 2048], replicated
- w_in: bfloat16 [2, 2048, 2, 4096], P(None, None, None, 'tp')
- conv_w: bfloat16 [2, 4, 4096], P(None, None, 'tp')
- conv_b: bfloat16 [2, 4096], P(None, 'tp')
- w_x: bfloat16 [2, 4096, 160], P(None, 'tp')
- w_dt: bfloat16 [2, 128, 4096], P(None, None, 'tp')
- b_dt: float32 [2, 4096], P(None, 'tp')
- a_log: float32 [2, 16, 4096], P(None, None, 'tp')
- d_skip: float32 [2, 4096], P(None, 'tp')
- w_out: bfloat16 [2, 4096, 2048], P(None, 'tp')
- conv_state: bfloat16 [2, 1024, 3, 4096], P(None, 'dp', None, 'tp'), parts along dimension 1
- ssm_state: float32 [2, 1024, 16, 4096], P(None, 'dp', None, 'tp'), parts along dimension 1
Outputs:
- output 1: float32 [1024, 2048], P('dp'), parts along dimension 0
- output 2: bfloat16 [2, 1024, 3, 4096], P(None, 'dp', None, 'tp'), parts along dimension 1
- output 3: float32 [2, 1024, 16, 4096], P(None, 'dp', None, 'tp'), parts along dimension 1
There are 4 independent parts. A program takes and returns all parts, laid end to end along the dimension named above; an argument that names none is the same for every part.
All inputs are finite; a program needn't handle non-finite values.
Results may differ from a plain program's by a relative error of at most 0.02.
Values are sent between devices in bfloat16 or wider.
A program may use at most 1 GiB of HBM per device.

v0:
```python
import jax
import jax.numpy as jnp
from jax import lax
from jax.sharding import PartitionSpec as P


def rms_norm(vector, epsilon):
    return vector * lax.rsqrt(jnp.mean(vector * vector, axis=-1, keepdims=True) + epsilon)


def solution(mesh):
    def device_step(residual, norm_w, w_in, conv_w, conv_b, w_x, w_dt, b_dt, a_log, d_skip, w_out, conv_state, ssm_state):
        rank_dim = w_dt.shape[1]
        state_dim = a_log.shape[1]
        conv_list = []
        ssm_list = []
        for layer_idx in range(norm_w.shape[0]):
            hidden = (rms_norm(residual, 1e-5) * norm_w[layer_idx].astype(jnp.float32)).astype(jnp.bfloat16)
            xz_val = jnp.einsum('bd,dwe->bwe', hidden, w_in[layer_idx], preferred_element_type=jnp.float32).astype(jnp.bfloat16)
            window = jnp.concatenate([conv_state[layer_idx], xz_val[:, 0:1, :]], axis=1)
            conv_pre = jnp.sum(window.astype(jnp.float32) * conv_w[layer_idx].astype(jnp.float32), axis=1) + conv_b[layer_idx].astype(jnp.float32)
            x_conv = jax.nn.silu(conv_pre).astype(jnp.bfloat16)
            proj_part = jnp.dot(x_conv, w_x[layer_idx], preferred_element_type=jnp.float32).astype(jnp.bfloat16)
            proj_sum = lax.psum(proj_part, 'tp').astype(jnp.float32)
            dt_low = rms_norm(proj_sum[:, :rank_dim], 1e-6).astype(jnp.bfloat16)
            b_vec = rms_norm(proj_sum[:, rank_dim:rank_dim + state_dim], 1e-6)
            c_vec = rms_norm(proj_sum[:, rank_dim + state_dim:], 1e-6)
            dt_val = jax.nn.softplus(jnp.dot(dt_low, w_dt[layer_idx], preferred_element_type=jnp.float32) + b_dt[layer_idx])
            x_float = x_conv.astype(jnp.float32)
            decay_fac = jnp.exp(dt_val[:, None, :] * -jnp.exp(a_log[layer_idx]))
            new_ssm = decay_fac * ssm_state[layer_idx] + (dt_val * x_float)[:, None, :] * b_vec[:, :, None]
            y_val = jnp.sum(new_ssm * c_vec[:, :, None], axis=1) + d_skip[layer_idx] * x_float
            gated_y = (y_val * jax.nn.silu(xz_val[:, 1, :].astype(jnp.float32))).astype(jnp.bfloat16)
            out_part = jnp.dot(gated_y, w_out[layer_idx], preferred_element_type=jnp.float32).astype(jnp.bfloat16)
            residual = residual + lax.psum(out_part, 'tp').astype(jnp.float32)
            conv_list.append(window[:, 1:, :])
            ssm_list.append(new_ssm)
        return residual, jnp.stack(conv_list), jnp.stack(ssm_list)

    cache_spec = P(None, 'dp', None, 'tp')
    in_specs = (P('dp', None), P(None, None), P(None, None, None, 'tp'), P(None, None, 'tp'), P(None, 'tp'), P(None, 'tp', None), P(None, None, 'tp'), P(None, 'tp'), P(None, None, 'tp'), P(None, 'tp'), P(None, 'tp', None), cache_spec, cache_spec)
    out_specs = (P('dp', None), cache_spec, cache_spec)
    return jax.shard_map(device_step, mesh=mesh, in_specs=in_specs, out_specs=out_specs, check_vma=False)
```

profile of v0, /device:TPU:0, one launch (start us, length us, event | category | flops | bytes accessed | tf_op | source)
XLA Modules:
  0.0 313.9 jit_solution(3060949591475670967)
XLA Ops:
  7.2 1.8 multiply_reduce_fusion.3
  9.0 1.3 slice_convert_fusion.2
  10.4 1.4 slice_convert_fusion.1
  11.8 1.3 bitcast_convert_fusion
  13.1 1.5 slice_bitcast_fusion
  14.6 8.3 %fusion.56 = (bf16[1,2048,2,512]{3,2,1,0:T(2,128)(2,1)S(1)}, bf16[1,2048,2,512]{3,2,1,0:T(2,128)(2,1)}) fusion(bf16[2,2048,2,512]{3,2,1,0:T(2,128)(2,1)} %param.15), kind=kLoop, calls=%fused_computation.126 | loop fusion | bytes 16777216 | tf_op jit(solution)/shard_map/slice | solution.py:19
  22.9 1.3 fusion.12
  24.2 0.2 multiply_reduce_fusion.2
  24.5 0.8 copy-done.8
  25.2 0.2 multiply_convert_fusion.5
  25.4 0.9 convolution_convert_fusion.3
  26.3 0.0 all-reduce.7.cloned.1.call-start
  26.4 0.6 fusion.58
  27.0 0.6 negate_bitcast_fusion
  27.6 0.6 fusion.57
  28.2 55.8 %all-reduce.5.cloned.1.call-done = bf16[256,160]{0,1:T(8,128)(2,1)} async-done(((bf16[256,160]{0,1:T(8,128)(2,1)}), bf16[256,160]{0,1:T(8,128)(2,1)}) %all-reduce.5.cloned.1.call-update) | async-done | bytes 81936 | tf_op jit(solution)/shard_map/psum | solution.py:24
  84.0 0.9 convert_element_type.133
  85.0 0.5 add_rsqrt_fusion.6
  85.5 0.6 slice_multiply_fusion.3
  86.1 0.8 copy.17
  86.9 0.8 copy.18
  87.7 1.5 convert_multiply_fusion.3
  89.2 7.9 %fusion.5 = f32[256,512]{1,0:T(8,128)S(1)} fusion(f32[2,256,16,512]{3,2,1,0:T(8,128)} %param.25, f32[256,16]{1,0:T(8,128)} %copy.18, f32[256,16]{1,0:T(8,128)S(1)} %copy.17, f32[256,512]{1,0:T(8,128)S(1)} %get-tuple-element.29, f32[16,512]{1,0:T(8,128)} %get-tuple-element.18, f32[256,512]{1,0:T(8,128)S(1)} %get-tuple-element.30), kind=kLoop, calls=%fused_computation.8 | loop fusion | flops 12451840 | bytes 10027008 | tf_op jit(solution)/shard_map/reduce_sum | solution.py:32
  97.2 1.9 convolution_convert_fusion.1
  99.2 2.0 fusion.25
  101.2 56.0 %all-reduce.7.cloned.1.call-done = bf16[256,2048]{1,0:T(8,128)(2,1)} async-done(((bf16[256,2048]{1,0:T(8,128)(2,1)}), bf16[256,2048]{1,0:T(8,128)(2,1)}) %all-reduce.7.cloned.1.call-update) | async-done | bytes 1048592 | tf_op jit(solution)/shard_map/psum | solution.py:35
  157.2 1.6 multiply_reduce_fusion.1
  158.8 3.8 %fusion.13 = bf16[256,2,512]{2,0,1:T(8,128)(2,1)S(1)} fusion(bf16[1,2048,2,512]{3,2,1,0:T(2,128)(2,1)} %get-tuple-element.10, f32[2048]{0:T(1024)S(1)} %bitcast.130, f32[256]{0:T(256)S(1)} %add_rsqrt_fusion.3, f32[256,2048]{1,0:T(8,128)S(1)} %copy-done, bf16[256,2048]{1,0:T(8,128)(2,1)} %all-reduce.7.cloned.1.call-done), kind=kOutput, calls=%fused_computation.37 | convolution fusion | flops 1076625408 | bytes 7873536 | tf_op jit(solution)/shard_map/bd,dwe->bwe/dot_general | solution.py:19
  162.7 0.9 fusion.23
  163.6 0.2 multiply_reduce_fusion
  163.9 0.8 copy-done.6
  164.6 0.2 multiply_convert_fusion.3
  164.8 0.9 convolution_convert_fusion.2
  165.7 0.2 all-reduce.11.cloned.1.call-start
  166.0 2.7 pad_maximum_fusion.1
  168.6 51.1 %all-reduce.9.cloned.1.call-done = bf16[256,160]{0,1:T(8,128)(2,1)} async-done(((bf16[256,160]{0,1:T(8,128)(2,1)}), bf16[256,160]{0,1:T(8,128)(2,1)}) %all-reduce.9.cloned.1.call-update) | async-done | bytes 81936 | tf_op jit(solution)/shard_map/psum | solution.py:24
  219.7 0.9 convert_element_type.148
  220.7 0.6 add_rsqrt_fusion.2
  221.3 0.6 slice_multiply_fusion.1
  221.9 0.8 copy.20
  222.7 0.1 copy.21
  222.8 1.7 convert_multiply_fusion.2
  224.6 16.0 %multiply_add_fusion.1 = (f32[1,256,16,512]{3,2,1,0:T(8,128)}, f32[1,256,16,512]{3,2,1,0:T(8,128)}) fusion(f32[2,256,16,512]{3,2,1,0:T(8,128)} %param.25, f32[256,16]{1,0:T(8,128)S(1)} %copy.17, f32[256,512]{1,0:T(8,128)S(1)} %copy-done.3, f32[16,512]{1,0:T(8,128)} %get-tuple-element.18, f32[256,512]{1,0:T(8,128)S(1)} %copy-done.5, f32[256,16]{1,0:T(8,128)S(1)} %copy.20, ...), kind=kLoop, calls=%fused_computation.10 | loop fusion | flops 16777216 | bytes 35749888 | tf_op jit(solution)/shard_map/add | solution.py:31
  240.7 3.3 %fusion.2 = f32[256,512]{1,0:T(8,128)S(1)} fusion(f32[2,256,16,512]{3,2,1,0:T(8,128)S(1)} %bitcast.125, f32[256,16]{1,0:T(8,128)S(1)} %copy.21, f32[256,16]{1,0:T(8,128)S(1)} %copy.20, f32[256,512]{1,0:T(8,128)S(1)} %get-tuple-element.31, f32[16,512]{1,0:T(8,128)S(1)} %copy-done.15, f32[256,512]{1,0:T(8,128)S(1)} %get-tuple-element.32), kind=kLoop, calls=%fused_computation.4 | loop fusion | flops 12451840 | bytes 10027008 | tf_op jit(solution)/shard_map/reduce_sum | solution.py:32
  244.1 1.9 convolution_convert_fusion
  246.0 12.5 %pad_maximum_fusion = f32[2,256,16,512]{3,2,1,0:T(8,128)} fusion(f32[1,256,16,512]{3,2,1,0:T(8,128)} %get-tuple-element.8, f32[1,256,16,512]{3,2,1,0:T(8,128)} %get-tuple-element.7), kind=kLoop, calls=%fused_computation | loop fusion | flops 4194304 | bytes 33554432 | tf_op jit(solution)/shard_map/stack | solution.py:38
  258.5 45.5 %all-reduce.11.cloned.1.call-done = bf16[256,2048]{1,0:T(8,128)(2,1)} async-done(((bf16[256,2048]{1,0:T(8,128)(2,1)}), bf16[256,2048]{1,0:T(8,128)(2,1)}) %all-reduce.11.cloned.1.call-update) | async-done | bytes 1048592 | tf_op jit(solution)/shard_map/psum | solution.py:35
  304.0 3.4 %convert_add_fusion = f32[256,2048]{1,0:T(8,128)} fusion(bf16[256,2048]{1,0:T(8,128)(2,1)} %all-reduce.11.cloned.1.call-done, f32[256,2048]{1,0:T(8,128)S(1)} %copy-done, bf16[256,2048]{1,0:T(8,128)(2,1)} %all-reduce.7.cloned.1.call-done), kind=kLoop, calls=%fused_computation.19 | loop fusion | flops 2097152 | bytes 6291456 | tf_op jit(solution)/shard_map/add | solution.py:35
  (90 shorter events, 0.5 us)
Async XLA Ops:
  7.2 76.8 %all-reduce.5.cloned.1.call-start = ((), (), s32[]{:S(2)}) async-start(), calls=%async_computation | async-start | bytes 163840 | tf_op jit(solution)/shard_map/psum | solution.py:24
  10.4 14.1 %copy-start.24 = (f32[1,512]{1,0:T(1,128)}, f32[1,512]{1,0:T(1,128)S(1)}, u32[]{:S(2)}) copy-start(f32[1,512]{1,0:T(1,128)S(1)} %get-tuple-element.28) | copy-start | bytes 6148
  14.5 9.7 %copy-start.1 = (bf16[256,3,512]{2,0,1:T(8,128)(2,1)}, bf16[256,3,512]{2,0,1:T(8,128)(2,1)S(1)}, u32[]{:S(2)}) copy-start(bf16[256,3,512]{2,0,1:T(8,128)(2,1)S(1)} %get-tuple-element.12) | copy-start | bytes 2359300
  14.5 8.3 %copy-start = (f32[256,2048]{1,0:T(8,128)S(1)}, f32[256,2048]{1,0:T(8,128)}, u32[]{:S(2)}) copy-start(f32[256,2048]{1,0:T(8,128)} %param.13) | copy-start | bytes 6291460
  22.8 2.6 copy-start.13
  22.8 3.6 %copy-start.27 = (f32[2,512]{1,0:T(2,128)S(1)}, f32[2,512]{1,0:T(2,128)}, u32[]{:S(2)}) copy-start(f32[2,512]{1,0:T(2,128)} %param.20) | copy-start | bytes 12292
  22.8 4.1 %copy-start.20 = (f32[2,16,512]{2,1,0:T(8,128)S(1)}, f32[2,16,512]{2,1,0:T(8,128)}, u32[]{:S(2)}) copy-start(f32[2,16,512]{2,1,0:T(8,128)} %param.21) | copy-start | bytes 196612
  22.8 4.8 %copy-start.28 = (f32[2,512]{1,0:T(2,128)S(1)}, f32[2,512]{1,0:T(2,128)}, u32[]{:S(2)}) copy-start(f32[2,512]{1,0:T(2,128)} %param.22) | copy-start | bytes 12292
  24.2 1.2 copy-start.18
  24.4 0.8 copy-start.8
  26.3 130.9 %all-reduce.7.cloned.1.call-start = ((), (), s32[]{:S(2)}) async-start(), calls=%async_computation.1 | async-start | bytes 2097152 | tf_op jit(solution)/shard_map/psum | solution.py:35
  84.9 1.2 copy-start.11
  89.2 8.0 %copy-start.2 = (f32[256,512]{1,0:T(8,128)}, f32[256,512]{1,0:T(8,128)S(1)}, u32[]{:S(2)}) copy-start(f32[256,512]{1,0:T(8,128)S(1)} %get-tuple-element.29) | copy-start | bytes 1572868
  89.2 8.0 %copy-start.4 = (f32[256,512]{1,0:T(8,128)}, f32[256,512]{1,0:T(8,128)S(1)}, u32[]{:S(2)}) copy-start(f32[256,512]{1,0:T(8,128)S(1)} %get-tuple-element.30) | copy-start | bytes 1572868
  89.2 8.0 %copy-start.9 = (f32[256,512]{1,0:T(8,128)S(1)}, f32[256,512]{1,0:T(8,128)}, u32[]{:S(2)}) copy-start(f32[256,512]{1,0:T(8,128)} %copy-done.8) | copy-start | bytes 1572868
  89.2 8.0 %copy-start.19 = (bf16[256,2,512]{2,0,1:T(8,128)(2,1)S(1)}, bf16[256,2,512]{2,0,1:T(8,128)(2,1)}, u32[]{:S(2)}) copy-start(bf16[256,2,512]{2,0,1:T(8,128)(2,1)} %copy-done.18) | copy-start | bytes 1572868
  89.2 8.0 %copy-start.25 = (f32[1,512]{1,0:T(1,128)S(1)}, f32[1,512]{1,0:T(1,128)}, u32[]{:S(2)}) copy-start(f32[1,512]{1,0:T(1,128)} %copy-done.24) | copy-start | bytes 6148
  89.2 8.0 %copy-start.30 = (f32[1,512]{1,0:T(1,128)S(1)}, f32[1,512]{1,0:T(1,128)}, u32[]{:S(2)}) copy-start(f32[1,512]{1,0:T(1,128)} %get-tuple-element.24) | copy-start | bytes 6148
  89.2 8.0 %copy-start.31 = (bf16[2,512,2048]{2,1,0:T(8,128)(2,1)S(1)}, bf16[2,512,2048]{2,1,0:T(8,128)(2,1)}, u32[]{:S(2)}) copy-start(bf16[2,512,2048]{2,1,0:T(8,128)(2,1)} %param.23) | copy-start | bytes 12582916
  99.1 59.7 %copy-start.26 = (f32[1,2048]{1,0:T(1,128)S(1)}, f32[1,2048]{1,0:T(1,128)}, u32[]{:S(2)}) copy-start(f32[1,2048]{1,0:T(1,128)} %get-tuple-element.22) | copy-start | bytes 24580
  99.1 120.6 %all-reduce.9.cloned.1.call-start = ((), (), s32[]{:S(2)}) async-start(), calls=%async_computation.2 | async-start | bytes 163840 | tf_op jit(solution)/shard_map/psum | solution.py:24
  158.8 4.8 %copy-start.21 = (f32[4,512]{1,0:T(4,128)S(1)}, f32[4,512]{1,0:T(4,128)}, u32[]{:S(2)}) copy-start(f32[4,512]{1,0:T(4,128)} %get-tuple-element.19) | copy-start | bytes 24580
  158.8 5.8 %copy-start.22 = (f32[1,512]{1,0:T(1,128)S(1)}, f32[1,512]{1,0:T(1,128)}, u32[]{:S(2)}) copy-start(f32[1,512]{1,0:T(1,128)} %get-tuple-element.27) | copy-start | bytes 6148
  162.6 2.2 copy-start.16
  162.6 2.2 copy-start.14
  163.6 60.9 %copy-start.3 = (f32[256,512]{1,0:T(8,128)S(1)}, f32[256,512]{1,0:T(8,128)}, u32[]{:S(2)}) copy-start(f32[256,512]{1,0:T(8,128)} %copy-done.2) | copy-start | bytes 1572868
  163.8 0.8 copy-start.6
  163.9 60.7 %copy-start.5 = (f32[256,512]{1,0:T(8,128)S(1)}, f32[256,512]{1,0:T(8,128)}, u32[]{:S(2)}) copy-start(f32[256,512]{1,0:T(8,128)} %copy-done.4) | copy-start | bytes 1572868
  164.8 57.1 %copy-start.10 = (bf16[256,512]{1,0:T(8,128)(2,1)}, bf16[256,512]{1,0:T(8,128)(2,1)S(1)}, u32[]{:S(2)}) copy-start(bf16[256,512]{1,0:T(8,128)(2,1)S(1)} %multiply_convert_fusion.3) | copy-start | bytes 786436
  165.7 138.3 %all-reduce.11.cloned.1.call-start = ((), (), s32[]{:S(2)}) async-start(), calls=%async_computation.3 | async-start | bytes 2097152 | tf_op jit(solution)/shard_map/psum | solution.py:35
  220.6 1.3 copy-start.12
  222.8 17.8 %slice-start = ((s8[16777216]{0:T(1024)(128)(4,1)}), s8[4194304]{0:T(1024)(128)(4,1)S(1)}, s32[]{:S(2)}) async-start(s8[16777216]{0:T(1024)(128)(4,1)} %bitcast.124), calls=%async_computation.4 | async-start | bytes 8388608
  224.6 16.1 %slice-start.1 = ((s8[16777216]{0:T(1024)(128)(4,1)}), s8[4194304]{0:T(1024)(128)(4,1)S(1)}, s32[]{:S(2)}) async-start(s8[16777216]{0:T(1024)(128)(4,1)} %bitcast.124), calls=%async_computation.5 | async-start | bytes 8388608
  224.6 16.1 %slice-start.2 = ((s8[16777216]{0:T(1024)(128)(4,1)}), s8[4194304]{0:T(1024)(128)(4,1)S(1)}, s32[]{:S(2)}) async-start(s8[16777216]{0:T(1024)(128)(4,1)} %bitcast.124), calls=%async_computation.6 | async-start | bytes 8388608
  224.6 16.1 %slice-start.3 = ((s8[16777216]{0:T(1024)(128)(4,1)}), s8[4194304]{0:T(1024)(128)(4,1)S(1)}, s32[]{:S(2)}) async-start(s8[16777216]{0:T(1024)(128)(4,1)} %bitcast.124), calls=%async_computation.7 | async-start | bytes 8388608
  224.6 16.1 %copy-start.15 = (f32[16,512]{1,0:T(8,128)S(1)}, f32[16,512]{1,0:T(8,128)}, u32[]{:S(2)}) copy-start(f32[16,512]{1,0:T(8,128)} %get-tuple-element.17) | copy-start | bytes 98308
  240.7 3.4 %copy-start.7 = (f32[256,512]{1,0:T(8,128)S(1)}, f32[256,512]{1,0:T(8,128)}, u32[]{:S(2)}) copy-start(f32[256,512]{1,0:T(8,128)} %copy-done.6) | copy-start | bytes 1572868
  240.7 3.4 %copy-start.17 = (bf16[256,2,512]{2,0,1:T(8,128)(2,1)S(1)}, bf16[256,2,512]{2,0,1:T(8,128)(2,1)}, u32[]{:S(2)}) copy-start(bf16[256,2,512]{2,0,1:T(8,128)(2,1)} %copy-done.16) | copy-start | bytes 1572868
  240.7 3.4 %copy-start.23 = (f32[1,512]{1,0:T(1,128)S(1)}, f32[1,512]{1,0:T(1,128)}, u32[]{:S(2)}) copy-start(f32[1,512]{1,0:T(1,128)} %get-tuple-element.27) | copy-start | bytes 6148
  240.7 3.4 %copy-start.29 = (f32[1,512]{1,0:T(1,128)S(1)}, f32[1,512]{1,0:T(1,128)}, u32[]{:S(2)}) copy-start(f32[1,512]{1,0:T(1,128)} %get-tuple-element.23) | copy-start | bytes 6148
  240.7 3.4 %copy-start.32 = (bf16[2,512,2048]{2,1,0:T(8,128)(2,1)S(1)}, bf16[2,512,2048]{2,1,0:T(8,128)(2,1)}, u32[]{:S(2)}) copy-start(bf16[2,512,2048]{2,1,0:T(8,128)(2,1)} %param.23) | copy-start | bytes 12582916
Sparse Core Ops, SparseCore 0:
  26.4 57.4 all-reduce.4
  99.3 57.8 all-reduce.6
  165.8 53.8 all-reduce.8
  246.1 57.8 all-reduce.10
where the time goes:
time: 315 us; the launch traced here: 314 us
  waiting for transfers between devices  208 us (66%)
  other arithmetic  61.8 us (20%)
  local copies, waits for them, and re-layouts  15.2 us (5%)
  between operations  14.4 us (5%)
  matrix products  13.8 us (4%)
    psum x2, waiting for transfers between devices, device_step(): proj_sum = lax.psum(proj_part, 'tp').astype(jnp.float32)  107 us
    psum x2, waiting for transfers between devices, device_step(): residual = residual + lax.psum(out_part, 'tp').astype(jnp.float32)  102 us
    another operation x4, other arithmetic, device_step(): return (residual, jnp.stack(conv_list), jnp.stack(ssm_list))  18.1 us
    add x1, other arithmetic, device_step(): decay_fac * ssm_state[layer_idx]  16 us
    reduce_sum x2, other arithmetic, device_step(): jnp.sum(new_ssm * c_vec[:, :, None], axis=1) + d_skip[layer_idx] * x_float  11.2 us
    slice x1, local copies, waits for them, and re-layouts, device_step(): w_in[layer_idx]  8.25 us
  transfers between devices with their start and end apart: 4, of which 4 were waited for; matrix products, arithmetic and copies ran while one was open for 6% of the time, Pallas kernels for 0%

commit v1 on v0

v1 whole, which is shorter than its diff:
```python
import functools

import jax
import jax.numpy as jnp
from jax import lax
from jax.experimental import pallas as pl
from jax.experimental.pallas import tpu as pltpu
from jax.sharding import PartitionSpec as P

MESH = pl.DeviceIdType.MESH
LOG2E = 1.4426950408889634
F32, BF16 = jnp.float32, jnp.bfloat16

ROWS = 256
D = 2048
E = 512
N = 16
RANK = 128
PW = RANK + 2 * N
NCH = 8
CR = ROWS // NCH
HALF = D // 2
KB = 8
KD = D // KB
OFF_B, OFF_C, OFF_D, OFF_E, OFF_F = 1, 3, 5, 7, 8


def silu(v):
    return v * jax.nn.sigmoid(v)


def rms(v, axis, eps):
    return v * lax.rsqrt(jnp.mean(v * v, axis=axis, keepdims=True) + eps)


def body(
    resid_in, norm_w, w_in, conv_w, conv_b, w_xt, w_dt, b_dt, a_log, d_skip, w_out, conv_in, ssm_in,
    resid, conv_out, ssm,
    v_norm, v_convw, v_convb, v_wxt, v_wdt, v_bdt, v_alog, v_dskip,
    w_raw, w_xz, s32, v_wout, conv0,
    hid, xcb, gate, dtb, dtx, dsx, bcb, a2,
    p_half, p_sa, p_ra, p_sb, p_rb, p_full,
    own, o_sa, o_ra, o_sb, o_rb, o_sc, o_rc, tot,
    small_sem, resid_sem, win_sem, conv_sem, ssm_sem, wout_sem,
    pa_send, pa_recv, pb_send, pb_recv, pf_send, pf_recv,
    a_send, a_recv, b_send, b_recv, c_send, c_recv, t_send, t_recv, f_send, f_recv,
):
    dp = lax.axis_index("dp")
    me = lax.axis_index("tp")
    core = lax.rem(me, 2)
    z = me // 2
    is_end = (z == 0) | (z == 3)
    is_mid = (z == 1) | (z == 2)
    partner = me + 1 - 2 * core
    zodd = lax.rem(z, 2)
    zpair = me + 2 - 4 * zodd
    midpeer = (3 - z) * 2 + core

    def dev(t):
        return (dp, t)

    def remote(src, dst, ssem, rsem, target):
        return pltpu.make_async_remote_copy(
            src_ref=src, dst_ref=dst, send_sem=ssem, recv_sem=rsem, device_id=dev(target), device_id_type=MESH)

    barrier = pltpu.get_barrier_semaphore()
    pl.semaphore_signal(barrier, inc=1, device_id=dev(partner), device_id_type=MESH)
    for k in range(1, 4):
        pl.semaphore_signal(barrier, inc=1, device_id=dev(lax.rem(me + 2 * k, 8)), device_id_type=MESH)

    copies = {}

    def load(key, src, dst, sem):
        c = pltpu.make_async_copy(src, dst, sem)
        c.start()
        copies[key] = c

    load("norm", norm_w, v_norm, small_sem.at[0])
    load("resid", resid_in, resid, resid_sem)
    for kb in range(KB):
        load(("win", 0, kb), w_in.at[0, pl.ds(kb * KD, KD)], w_raw.at[0, pl.ds(kb * KD, KD)], win_sem.at[0, kb])
    small = ((conv_w, v_convw), (conv_b, v_convb), (w_xt, v_wxt), (w_dt, v_wdt), (b_dt, v_bdt), (a_log, v_alog), (d_skip, v_dskip))
    for i, (s, d) in enumerate(small):
        load(("small", i), s, d, small_sem.at[i + 1])
    load(("conv0", 0), conv_in.at[0, 0], conv0.at[0], conv_sem.at[0])
    load(("conv", 0), conv_in.at[0, pl.ds(1, 2)], conv_out.at[0, pl.ds(0, 2)], conv_sem.at[1])
    load(("ssm", 0), ssm_in.at[0], ssm.at[0], ssm_sem.at[0])
    load(("wout", 0), w_out.at[0], v_wout.at[0], wout_sem.at[0])
    for kb in range(KB):
        load(("win", 1, kb), w_in.at[1, pl.ds(kb * KD, KD)], w_raw.at[1, pl.ds(kb * KD, KD)], win_sem.at[1, kb])
    load(("conv0", 1), conv_in.at[1, 0], conv0.at[1], conv_sem.at[2])
    load(("conv", 1), conv_in.at[1, pl.ds(1, 2)], conv_out.at[1, pl.ds(0, 2)], conv_sem.at[3])
    load(("ssm", 1), ssm_in.at[1], ssm.at[1], ssm_sem.at[1])
    load(("wout", 1), w_out.at[1], v_wout.at[1], wout_sem.at[1])

    def make_hidden(l):
        nw = v_norm[...].astype(F32)[l:l + 1, :]

        def step(i, c):
            rows = pl.ds(pl.multiple_of(i * CR, CR), CR)
            hid[rows, :] = (rms(resid[rows, :], 1, 1e-5) * nw).astype(BF16)
            return c

        lax.fori_loop(0, NCH, step, 0)

    def split_weights(l):
        for kb in range(KB):
            copies["win", l, kb].wait()

        def step(kb, c):
            rows = pl.ds(pl.multiple_of(kb * KD, KD), KD)
            for j in range(4):
                s32[j] = w_raw[l, rows, :, j * 128:(j + 1) * 128].reshape(2 * KD, 128).astype(F32)
            for w in range(2):
                for j in range(4):
                    w_xz[w, rows, j * 128:(j + 1) * 128] = s32[j, pl.ds(w, KD, stride=2), :].astype(BF16)
            return c

        lax.fori_loop(0, KB, step, 0)

    def front(l):
        x_b = jnp.dot(hid[...], w_xz[0], preferred_element_type=F32).astype(BF16)
        conv_out[l, 2] = x_b
        gate[...] = silu(jnp.dot(hid[...], w_xz[1], preferred_element_type=F32).astype(BF16).astype(F32))
        copies["conv0", l].wait()
        copies["conv", l].wait()
        cw = v_convw[l].astype(F32)
        pre = v_convb[...].astype(F32)[l:l + 1, :] + cw[3:4, :] * conv_out[l, 2].astype(F32)
        pre = pre + cw[0:1, :] * conv0[l].astype(F32)
        pre = pre + cw[1:2, :] * conv_out[l, 0].astype(F32)
        pre = pre + cw[2:3, :] * conv_out[l, 1].astype(F32)
        xcb[...] = silu(pre).astype(BF16)
        dsx[...] = v_dskip[...][l:l + 1, :] * xcb[...].astype(F32)
        pt = lax.dot_general(v_wxt[l], xcb[...], (((1,), (1,)), ((), ())), preferred_element_type=F32)
        p_half[0] = pt[:, :128]
        p_half[1] = pt[:, 128:]

    def p_sum(l, between):
        p_sa[...] = p_half[1 - core].astype(BF16)
        ca = remote(p_sa, p_ra.at[l], pa_send.at[l], pa_recv.at[l], partner)
        ca.start()
        ca.wait()
        p_sb[...] = (p_half[core] + p_ra[l].astype(F32)).astype(BF16)
        cb = []
        for k in range(1, 4):
            cb.append(remote(p_sb, p_rb.at[l, k - 1], pb_send.at[l, k - 1], pb_recv.at[l, k - 1], lax.rem(me + 2 * k, 8)))
            cb[-1].start()
        between()
        for c in cb:
            c.wait()
        total = jnp.zeros((PW, 128), F32)
        mine = p_sb[...].astype(F32)
        got = [p_rb[l, k].astype(F32) for k in range(3)]
        for chip in range(4):
            d = lax.rem(z - chip + 4, 4)
            term = jnp.where(d == 0, mine, jnp.where(d == 1, got[0], jnp.where(d == 2, got[1], got[2])))
            total = total + term
        p_full[l, core] = total
        cf = remote(p_full.at[l, core], p_full.at[l, core], pf_send.at[l], pf_recv.at[l], partner)
        cf.start()
        cf.wait()

    def steps(l):
        a2[...] = -jnp.exp(v_alog[l]) * LOG2E
        for h in range(2):
            rows = pl.ds(h * 128, 128)
            pt = p_full[l, h]
            low = rms(pt[:RANK].T, 1, 1e-6).astype(BF16)
            lin = jnp.dot(low, v_wdt[l], preferred_element_type=F32) + v_bdt[...][l:l + 1, :]
            dt = jnp.maximum(lin, 0.0) + jnp.log1p(jnp.exp(-jnp.abs(lin)))
            dtb[rows, :] = dt
            dtx[rows, :] = dt * xcb[rows, :].astype(F32)
            b = rms(pt[RANK:RANK + N], 0, 1e-6)
            c = rms(pt[RANK + N:], 0, 1e-6)
            bc = jnp.concatenate([b, c, jnp.zeros((128 - 2 * N, 128), F32)], axis=0)
            bcb[rows, :] = bc.T

    def stage_a(l, i):
        lane = lax.broadcasted_iota(jnp.int32, (1, N, 128), 2)
        sub = lax.broadcasted_iota(jnp.int32, (1, N, 128), 1)
        pick_b = lane == sub
        pick_c = lane == sub + N
        r0 = pl.multiple_of(i * CR, CR)

        def rows8(g, c):
            b0 = pl.multiple_of(r0 + g * 8, 8)
            bc = jnp.broadcast_to(bcb[pl.ds(b0, 8), :][:, None, :], (8, N, 128))
            bcol = jnp.sum(jnp.where(pick_b, bc, 0.0), axis=2, keepdims=True)
            ccol = jnp.sum(jnp.where(pick_c, bc, 0.0), axis=2, keepdims=True)
            for j in range(4):
                cols = pl.ds(j * 128, 128)
                dt8 = dtb[pl.ds(b0, 8), cols]
                dx8 = dtx[pl.ds(b0, 8), cols]
                decay = jnp.exp2(dt8[:, None, :] * a2[:, cols][None])
                new = decay * ssm[l, pl.ds(b0, 8), :, cols] + dx8[:, None, :] * bcol
                ssm[l, pl.ds(b0, 8), :, cols] = new
                y = jnp.sum(new * ccol, axis=1) + dsx[pl.ds(b0, 8), cols]
                gate[pl.ds(b0, 8), cols] = y * gate[pl.ds(b0, 8), cols]
            return c

        lax.fori_loop(0, CR // 8, rows8, 0)
        yg = gate[pl.ds(r0, CR), :].astype(BF16)
        theirs = pl.ds(pl.multiple_of((1 - core) * HALF, HALF), HALF)
        ours = pl.ds(pl.multiple_of(core * HALF, HALF), HALF)
        o_sa[i] = jnp.dot(yg, v_wout[l, :, theirs], preferred_element_type=F32).astype(BF16)
        copy_a(l, i).start()
        own[i] = jnp.dot(yg, v_wout[l, :, ours], preferred_element_type=F32)

    def copy_a(l, i):
        return remote(o_sa.at[i], o_ra.at[l, i], a_send.at[i], a_recv.at[i], partner)

    def copy_b(l, i):
        return remote(o_sb.at[i], o_rb.at[l, i], b_send.at[i], b_recv.at[i], zpair)

    def copy_c(l, i):
        return remote(o_sc.at[i], o_rc.at[l, i], c_send.at[i], c_recv.at[i], midpeer)

    def copy_t(l, i):
        return remote(tot.at[l, core, i], tot.at[l, core, i], t_send.at[i], t_recv.at[i], zpair)

    def copy_f(l, i):
        return remote(tot.at[l, core, i], tot.at[l, core, i], f_send.at[i], f_recv.at[i], partner)

    def stage_b(l, i):
        copy_a(l, i).wait()
        chip = own[i] + o_ra[l, i].astype(F32)

        @pl.when(is_end)
        def _():
            o_sb[i] = chip.astype(BF16)
            copy_b(l, i).start()

        @pl.when(is_mid)
        def _():
            own[i] = chip

    def stage_c(l, i):
        @pl.when(is_mid)
        def _():
            copy_b(l, i).wait_recv()
            o_sc[i] = (own[i] + o_rb[l, i].astype(F32)).astype(BF16)
            copy_c(l, i).start()

        @pl.when(is_end)
        def _():
            copy_b(l, i).wait_send()

    def stage_d(l, i):
        @pl.when(is_mid)
        def _():
            copy_c(l, i).wait()
            tot[l, core, i] = (o_sc[i].astype(F32) + o_rc[l, i].astype(F32)).astype(BF16)
            copy_t(l, i).start()
            copy_f(l, i).start()

    def stage_e(l, i):
        @pl.when(is_end)
        def _():
            copy_t(l, i).wait_recv()
            copy_f(l, i).start()

        @pl.when(is_mid)
        def _():
            copy_t(l, i).wait_send()

    def stage_f(l, i):
        copy_f(l, i).wait()
        rows = pl.ds(pl.multiple_of(i * CR, CR), CR)
        resid[rows, :HALF] = resid[rows, :HALF] + tot[l, 0, i].astype(F32)
        resid[rows, HALF:] = resid[rows, HALF:] + tot[l, 1, i].astype(F32)

    def back(l):
        copies["ssm", l].wait()
        copies["wout", l].wait()

        def step(t, c):
            for off, stage in ((0, stage_a), (OFF_B, stage_b), (OFF_C, stage_c), (OFF_D, stage_d), (OFF_E, stage_e), (OFF_F, stage_f)):
                @pl.when((t >= off) & (t < off + NCH))
                def _():
                    stage(l, t - off)
            return c

        lax.fori_loop(0, NCH + OFF_F, step, 0)

    copies["norm"].wait()
    copies["resid"].wait()
    make_hidden(0)
    split_weights(0)
    for i in range(len(small)):
        copies["small", i].wait()
    front(0)
    pl.semaphore_wait(barrier, 4)
    p_sum(0, lambda: split_weights(1))
    steps(0)
    back(0)
    make_hidden(1)
    front(1)
    p_sum(1, lambda: None)
    steps(1)
    back(1)


def solution(mesh):
    hbm = pl.BlockSpec(memory_space=pl.ANY)
    vmem = pl.BlockSpec(memory_space=pltpu.VMEM)
    V = pltpu.VMEM
    dma = pltpu.SemaphoreType.DMA

    def device_step(residual, norm_w, w_in, conv_w, conv_b, w_x, w_dt, b_dt, a_log, d_skip, w_out, conv_state, ssm_state):
        conv_t = jnp.transpose(conv_state, (0, 2, 1, 3))
        w_xt = jnp.transpose(w_x, (0, 2, 1))
        scratch = [
            V((2, D), BF16), V((2, 4, E), BF16), V((2, E), BF16), V((2, PW, E), BF16), V((2, RANK, E), BF16),
            V((2, E), F32), V((2, N, E), F32), V((2, E), F32),
            V((2, D, 2, E), BF16), V((2, D, E), BF16), V((4, 2 * KD, 128), F32), V((2, E, D), BF16), V((2, ROWS, E), BF16),
            V((ROWS, D), BF16), V((ROWS, E), BF16), V((ROWS, E), F32), V((ROWS, E), F32), V((ROWS, E), F32), V((ROWS, E), F32),
            V((ROWS, 128), F32), V((N, E), F32),
            V((2, PW, 128), F32), V((PW, 128), BF16), V((2, PW, 128), BF16), V((PW, 128), BF16), V((2, 3, PW, 128), BF16),
            V((2, 2, PW, 128), F32),
            V((NCH, CR, HALF), F32), V((NCH, CR, HALF), BF16), V((2, NCH, CR, HALF), BF16), V((NCH, CR, HALF), BF16),
            V((2, NCH, CR, HALF), BF16), V((NCH, CR, HALF), BF16), V((2, NCH, CR, HALF), BF16), V((2, 2, NCH, CR, HALF), BF16),
            dma((8,)), dma, dma((2, KB)), dma((4,)), dma((2,)), dma((2,)),
            dma((2,)), dma((2,)), dma((2, 3)), dma((2, 3)), dma((2,)), dma((2,)),
        ] + [dma((NCH,))] * 10
        resid, conv_out, ssm = pl.pallas_call(
            body,
            out_shape=(V((ROWS, D), F32), V((2, 3, ROWS, E), BF16), V((2, ROWS, N, E), F32)),
            in_specs=[hbm] * 13,
            out_specs=(vmem, vmem, vmem),
            scratch_shapes=scratch,
            compiler_params=pltpu.CompilerParams(collective_id=0, has_side_effects=True, vmem_limit_bytes=42 * 1024 * 1024),
        )(residual, norm_w, w_in, conv_w, conv_b, w_xt, w_dt, b_dt, a_log, d_skip, w_out, conv_t, ssm_state)
        return resid, jnp.transpose(conv_out, (0, 2, 1, 3)), ssm

    cache_spec = P(None, 'dp', None, 'tp')
    in_specs = (P('dp', None), P(None, None), P(None, None, None, 'tp'), P(None, None, 'tp'), P(None, 'tp'), P(None, 'tp', None), P(None, None, 'tp'), P(None, 'tp'), P(None, None, 'tp'), P(None, 'tp'), P(None, 'tp', None), cache_spec, cache_spec)
    out_specs = (P('dp', None), cache_spec, cache_spec)
    return jax.shard_map(device_step, mesh=mesh, in_specs=in_specs, out_specs=out_specs, check_vma=False)
```

time: 315 us -> 94.6 us (0.30)
  waiting for transfers between devices: 208 us -> 0 us
  Pallas kernels: 0 us -> 85.2 us
  other arithmetic: 61.8 us -> 0 us
  matrix products: 13.8 us -> 0 us
  between operations: 14.4 us -> 0.64 us
  local copies, waits for them, and re-layouts: 15.2 us -> 8.62 us
    psum x4 -> x0, waiting for transfers between devices: 208 us -> none  [the longest x2 107 us: device_step(): proj_sum = lax.psum(proj_part, 'tp').astype(jnp.float32)]
    pallas_call x0 -> x1, Pallas kernels: none -> 85.2 us  [device_step(): pl.pallas_call(body, out_shape=(V((ROWS, D), F32), V((2, 3, ROWS, E), BF1...]
    add x3 -> x0, other arithmetic: 20.7 us -> none  [the longest x1 16 us: device_step(): decay_fac * ssm_state[layer_idx]]
    another operation x4 -> x0, other arithmetic: 18.1 us -> none  [device_step(): return (residual, jnp.stack(conv_list), jnp.stack(ssm_list))]
    reduce_sum x10 -> x0, other arithmetic: 15.2 us -> none  [the longest x2 11.2 us: device_step(): jnp.sum(new_ssm * c_vec[:, :, None], axis=1) + d_skip[layer_idx] * x_float]
    dot_general x8 -> x0, matrix products: 13.8 us -> none  [the longest x2 5.12 us: device_step(): jnp.einsum('bd,dwe->bwe', hidden, w_in[layer_idx], preferred_element_type...]
    slice x5 -> x0, local copies, waits for them, and re-layouts: 9.48 us -> none  [the longest x1 8.25 us: device_step(): w_in[layer_idx]]
    unnamed x74 -> x3, local copies, waits for them, and re-layouts: 1.73 us -> 8.62 us
  transfers between devices with their start and end apart: 4 -> 0, of which waited for: 4 -> 0; matrix products, arithmetic and copies ran while one was open for 6% -> 0% of each run, Pallas kernels for 0% -> 0%
where the time goes in v1:
time: 94.6 us; the launch traced here: 94.4 us
  Pallas kernels  85.2 us (90%)
  local copies, waits for them, and re-layouts  8.62 us (9%)
    pallas_call x1, Pallas kernels, device_step(): pl.pallas_call(body, out_shape=(V((ROWS, D), F32), V((2, 3, ROWS, E), BF1...  85.2 us
    unnamed x3, local copies, waits for them, and re-layouts  8.62 us

profile of v1, /device:TPU:0, one launch (start us, length us, event | category | flops | bytes accessed | tf_op | source)
XLA Modules:
  0.0 94.4 jit_solution(4603719745081734954)
XLA Ops:
  0.6 85.2 %shard_map.148 = (f32[256,2048]{1,0:T(8,128)S(1)}, bf16[2,3,256,512]{3,2,1,0:T(8,128)(2,1)S(1)}, f32[2,256,16,512]{3,2,1,0:T(8,128)S(1)}) custom-call(f32[256,2048]{1,0:T(8,128)} %resid_in.1, bf16[2,2048]{1,0:T(2,128)(2,1)} %norm_w.1, bf16[2,2048,2,512]{3,2,1,0:T(2,128)(2,1)} %w_in.1, bf16[2,4,512]{2,1,0:T(4,128)(2,1)} %conv_w.1, bf16[2,512]{1,0:T(2,128)(2,1)} %conv_b.1, ...), custom_call_target="tpu_custom_call" | custom-call | tf_op jit(solution)/shard_map/pallas_call | solution.py:325
  85.8 1.3 %copy.19 = f32[256,2048]{1,0:T(8,128)} copy(f32[256,2048]{1,0:T(8,128)S(1)} %get-tuple-element.9) | data formatting | bytes 4194304
  87.1 1.1 %copy.20 = bf16[2,256,3,512]{3,1,2,0:T(8,128)(2,1)} copy(bf16[2,256,3,512]{3,1,2,0:T(8,128)(2,1)S(1)} %bitcast.3) | data formatting | bytes 3145728
  88.3 6.2 %copy.21 = f32[2,256,16,512]{3,2,1,0:T(8,128)} copy(f32[2,256,16,512]{3,2,1,0:T(8,128)S(1)} %get-tuple-element.11) | data formatting | bytes 33554432

commit v2 on v1

v2 whole, which is shorter than its diff:
```python
import functools

import jax
import jax.numpy as jnp
from jax import lax
from jax.experimental import pallas as pl
from jax.experimental.pallas import tpu as pltpu
from jax.sharding import PartitionSpec as P

MESH = pl.DeviceIdType.MESH
LOG2E = 1.4426950408889634
F32, BF16 = jnp.float32, jnp.bfloat16

ROWS = 256
D = 2048
E = 512
N = 16
RANK = 128
PW = RANK + 2 * N
NCH = 8
CR = ROWS // NCH
HALF = D // 2
KB = 8
KD = D // KB
HR = ROWS // 2
HC = NCH // 2
PH = PW // 2
SPLIT_EARLY = 6
OFF_B, OFF_C, OFF_D, OFF_E, OFF_F = 1, 3, 5, 7, 8
T_FRONT = HC - 1 + OFF_F
P_WAIT = 4
NEXT = T_FRONT + P_WAIT + 1


def silu(v):
    return v * jax.nn.sigmoid(v)


def rms(v, axis, eps):
    return v * lax.rsqrt(jnp.mean(v * v, axis=axis, keepdims=True) + eps)


def body(
    resid_in, norm_w, w_in, conv_w, conv_b, w_xt, w_dt, b_dt, a_log, d_skip, w_out, conv_in, ssm_in,
    resid, conv_out, ssm,
    v_norm, v_convw, v_convb, v_wxt, v_wdt, v_bdt, v_alog, v_dskip,
    w_raw, w_xz, s32, v_wout, conv0,
    hid, xcb, gate, dtb, dtx, dsx, bcb, a2,
    p_own, p_sa, p_ra, p_sb, p_rb, p_full,
    own, o_sa, o_ra, o_sb, o_rb, o_sc, o_rc, tot,
    small_sem, resid_sem, win_sem, conv_sem, ssm_sem, wout_sem,
    pa_send, pa_recv, pb_send, pb_recv, pf_send, pf_recv,
    a_send, a_recv, b_send, b_recv, c_send, c_recv, t_send, t_recv, f_send, f_recv,
):
    dp = lax.axis_index("dp")
    me = lax.axis_index("tp")
    core = lax.rem(me, 2)
    z = me // 2
    is_end = (z == 0) | (z == 3)
    is_mid = (z == 1) | (z == 2)
    partner = me + 1 - 2 * core
    zodd = lax.rem(z, 2)
    zpair = me + 2 - 4 * zodd
    midpeer = (3 - z) * 2 + core

    def dev(t):
        return (dp, t)

    def remote(src, dst, ssem, rsem, target):
        return pltpu.make_async_remote_copy(
            src_ref=src, dst_ref=dst, send_sem=ssem, recv_sem=rsem, device_id=dev(target), device_id_type=MESH)

    barrier = pltpu.get_barrier_semaphore()
    pl.semaphore_signal(barrier, inc=1, device_id=dev(partner), device_id_type=MESH)
    for k in range(1, 4):
        pl.semaphore_signal(barrier, inc=1, device_id=dev(lax.rem(me + 2 * k, 8)), device_id_type=MESH)

    copies = {}

    def load(key, src, dst, sem):
        c = pltpu.make_async_copy(src, dst, sem)
        c.start()
        copies[key] = c

    def wait(key):
        copies.pop(key).wait()

    def load_win(l):
        for kb in range(KB):
            load(("win", l, kb), w_in.at[l, pl.ds(kb * KD, KD)], w_raw.at[l, pl.ds(kb * KD, KD)], win_sem.at[l, kb])

    def load_conv(l):
        load(("conv0", l), conv_in.at[l, 0], conv0.at[l], conv_sem.at[2 * l])
        load(("conv", l), conv_in.at[l, pl.ds(1, 2)], conv_out.at[l, pl.ds(0, 2)], conv_sem.at[2 * l + 1])

    def load_state(l):
        load(("wout", l), w_out.at[l], v_wout.at[l], wout_sem.at[l])
        load(("ssm", l), ssm_in.at[l], ssm.at[l], ssm_sem.at[l])

    load("norm", norm_w, v_norm, small_sem.at[0])
    load("resid", resid_in, resid, resid_sem)
    load_win(0)
    small = ((conv_w, v_convw), (conv_b, v_convb), (w_xt, v_wxt), (w_dt, v_wdt), (b_dt, v_bdt), (a_log, v_alog), (d_skip, v_dskip))
    for i, (s, d) in enumerate(small):
        load(("small", i), s, d, small_sem.at[i + 1])
    load_conv(0)

    def row_of(ref, l):
        v = ref[...].astype(F32)
        return jnp.where(l == 0, v[0:1, :], v[1:2, :])

    def split_block(l, kb):
        rows = pl.ds(pl.multiple_of(kb * KD, KD), KD)
        for j in range(4):
            s32[j] = w_raw[l, rows, :, j * 128:(j + 1) * 128].reshape(2 * KD, 128).astype(F32)
        for w in range(2):
            for j in range(4):
                w_xz[w, rows, j * 128:(j + 1) * 128] = s32[j, pl.ds(w, KD, stride=2), :].astype(BF16)

    def split_blocks(l, lo, hi):
        def step(kb, c):
            split_block(l, kb)
            return c

        lax.fori_loop(lo, hi, step, 0)

    def hidden(l, h):
        nw = row_of(v_norm, l)

        def step(i, c):
            rows = pl.ds(pl.multiple_of(h * HR + i * CR, CR), CR)
            hid[rows, :] = (rms(resid[rows, :], 1, 1e-5) * nw).astype(BF16)
            return c

        lax.fori_loop(0, HR // CR, step, 0)

    def front(l, h):
        rows = pl.ds(pl.multiple_of(h * HR, HR), HR)
        x_b = jnp.dot(hid[rows, :], w_xz[0], preferred_element_type=F32).astype(BF16)
        conv_out[l, 2, rows, :] = x_b
        gate[rows, :] = silu(jnp.dot(hid[rows, :], w_xz[1], preferred_element_type=F32).astype(BF16).astype(F32))
        cw = v_convw[l].astype(F32)
        pre = row_of(v_convb, l) + cw[3:4, :] * conv_out[l, 2, rows, :].astype(F32)
        pre = pre + cw[0:1, :] * conv0[l, rows, :].astype(F32)
        pre = pre + cw[1:2, :] * conv_out[l, 0, rows, :].astype(F32)
        pre = pre + cw[2:3, :] * conv_out[l, 1, rows, :].astype(F32)
        xcb[rows, :] = silu(pre).astype(BF16)
        dsx[rows, :] = row_of(v_dskip, l) * xcb[rows, :].astype(F32)
        p_own[h] = lax.dot_general(v_wxt[l], xcb[rows, :], (((1,), (1,)), ((), ())), preferred_element_type=F32)

    mine = pl.ds(pl.multiple_of(core * PH, PH), PH)
    theirs = pl.ds(pl.multiple_of((1 - core) * PH, PH), PH)

    def copy_pa(l, h):
        return remote(p_sa.at[h], p_ra.at[l, h], pa_send.at[l, h], pa_recv.at[l, h], partner)

    def copy_pb(l, h, k):
        return remote(p_sb.at[h], p_rb.at[l, h, k - 1], pb_send.at[l, h, k - 1], pb_recv.at[l, h, k - 1], lax.rem(me + 2 * k, 8))

    def copy_pf(l, h):
        return remote(p_full.at[l, h, mine], p_full.at[l, h, mine], pf_send.at[l, h], pf_recv.at[l, h], partner)

    def p_one(l, h):
        p_sa[h] = p_own[h, theirs, :].astype(BF16)
        copy_pa(l, h).start()

    def p_two(l, h):
        copy_pa(l, h).wait()
        p_sb[h] = (p_own[h, mine, :] + p_ra[l, h].astype(F32)).astype(BF16)
        for k in range(1, 4):
            copy_pb(l, h, k).start()

    def p_three(l, h):
        for k in range(1, 4):
            copy_pb(l, h, k).wait()
        total = jnp.zeros((PH, HR), F32)
        parts = [p_sb[h].astype(F32)] + [p_rb[l, h, k].astype(F32) for k in range(3)]
        for chip in range(4):
            d = lax.rem(z - chip + 4, 4)
            total = total + jnp.where(d == 0, parts[0], jnp.where(d == 1, parts[1], jnp.where(d == 2, parts[2], parts[3])))
        p_full[l, h, mine, :] = total
        copy_pf(l, h).start()

    def p_four(l, h):
        copy_pf(l, h).wait()
        a2[...] = -jnp.exp(v_alog[l]) * LOG2E
        rows = pl.ds(pl.multiple_of(h * HR, HR), HR)
        pt = p_full[l, h]
        low = rms(pt[:RANK].T, 1, 1e-6).astype(BF16)
        lin = jnp.dot(low, v_wdt[l], preferred_element_type=F32) + row_of(v_bdt, l)
        dt = jnp.maximum(lin, 0.0) + jnp.log1p(jnp.exp(-jnp.abs(lin)))
        dtb[rows, :] = dt
        dtx[rows, :] = dt * xcb[rows, :].astype(F32)
        b = rms(pt[RANK:RANK + N], 0, 1e-6)
        c = rms(pt[RANK + N:], 0, 1e-6)
        bc = jnp.concatenate([b, c, jnp.zeros((128 - 2 * N, HR), F32)], axis=0)
        bcb[rows, :] = bc.T

    def stage_a(l, i):
        lane = lax.broadcasted_iota(jnp.int32, (1, N, 128), 2)
        sub = lax.broadcasted_iota(jnp.int32, (1, N, 128), 1)
        pick_b = lane == sub
        pick_c = lane == sub + N
        r0 = pl.multiple_of(i * CR, CR)

        def rows8(g, c):
            b0 = pl.multiple_of(r0 + g * 8, 8)
            bc = jnp.broadcast_to(bcb[pl.ds(b0, 8), :][:, None, :], (8, N, 128))
            bcol = jnp.sum(jnp.where(pick_b, bc, 0.0), axis=2, keepdims=True)
            ccol = jnp.sum(jnp.where(pick_c, bc, 0.0), axis=2, keepdims=True)
            for j in range(4):
                cols = pl.ds(j * 128, 128)
                dt8 = dtb[pl.ds(b0, 8), cols]
                dx8 = dtx[pl.ds(b0, 8), cols]
                decay = jnp.exp2(dt8[:, None, :] * a2[:, cols][None])
                new = decay * ssm[l, pl.ds(b0, 8), :, cols] + dx8[:, None, :] * bcol
                ssm[l, pl.ds(b0, 8), :, cols] = new
                y = jnp.sum(new * ccol, axis=1) + dsx[pl.ds(b0, 8), cols]
                gate[pl.ds(b0, 8), cols] = y * gate[pl.ds(b0, 8), cols]
            return c

        lax.fori_loop(0, CR // 8, rows8, 0)
        yg = gate[pl.ds(r0, CR), :].astype(BF16)
        their_cols = pl.ds(pl.multiple_of((1 - core) * HALF, HALF), HALF)
        our_cols = pl.ds(pl.multiple_of(core * HALF, HALF), HALF)
        o_sa[i] = jnp.dot(yg, v_wout[l, :, their_cols], preferred_element_type=F32).astype(BF16)
        copy_a(l, i).start()
        own[i] = jnp.dot(yg, v_wout[l, :, our_cols], preferred_element_type=F32)

    def copy_a(l, i):
        return remote(o_sa.at[i], o_ra.at[l, i], a_send.at[l, i], a_recv.at[l, i], partner)

    def copy_b(l, i):
        return remote(o_sb.at[i], o_rb.at[l, i], b_send.at[l, i], b_recv.at[l, i], zpair)

    def copy_c(l, i):
        return remote(o_sc.at[i], o_rc.at[l, i], c_send.at[l, i], c_recv.at[l, i], midpeer)

    def copy_t(l, i):
        return remote(tot.at[l, core, i], tot.at[l, core, i], t_send.at[l, i], t_recv.at[l, i], zpair)

    def copy_f(l, i):
        return remote(tot.at[l, core, i], tot.at[l, core, i], f_send.at[l, i], f_recv.at[l, i], partner)

    def stage_b(l, i):
        copy_a(l, i).wait()
        chip = own[i] + o_ra[l, i].astype(F32)

        @pl.when(is_end)
        def _():
            o_sb[i] = chip.astype(BF16)
            copy_b(l, i).start()

        @pl.when(is_mid)
        def _():
            own[i] = chip

    def stage_c(l, i):
        @pl.when(is_mid)
        def _():
            copy_b(l, i).wait_recv()
            o_sc[i] = (own[i] + o_rb[l, i].astype(F32)).astype(BF16)
            copy_c(l, i).start()

        @pl.when(is_end)
        def _():
            copy_b(l, i).wait_send()

    def stage_d(l, i):
        @pl.when(is_mid)
        def _():
            copy_c(l, i).wait()
            tot[l, core, i] = (o_sc[i].astype(F32) + o_rc[l, i].astype(F32)).astype(BF16)
            copy_t(l, i).start()
            copy_f(l, i).start()

    def stage_e(l, i):
        @pl.when(is_end)
        def _():
            copy_t(l, i).wait_recv()
            copy_f(l, i).start()

        @pl.when(is_mid)
        def _():
            copy_t(l, i).wait_send()

    def stage_f(l, i):
        copy_f(l, i).wait()
        rows = pl.ds(pl.multiple_of(i * CR, CR), CR)
        resid[rows, :HALF] = resid[rows, :HALF] + tot[l, 0, i].astype(F32)
        resid[rows, HALF:] = resid[rows, HALF:] + tot[l, 1, i].astype(F32)

    wait("norm")
    wait("resid")
    hidden(0, 0)
    hidden(0, 1)
    for kb in range(KB):
        wait(("win", 0, kb))
    split_blocks(0, 0, KB)
    load_win(1)
    load_state(0)
    load_conv(1)
    load_state(1)
    for i in range(len(small)):
        wait(("small", i))
    wait(("conv0", 0))
    wait(("conv", 0))

    def first(h, c):
        front(0, h)

        @pl.when(h == 0)
        def _():
            pl.semaphore_wait(barrier, 4)

        p_one(0, h)
        return c

    lax.fori_loop(0, 2, first, 0)
    p_two(0, 0)
    p_two(0, 1)
    for kb in range(KB):
        wait(("win", 1, kb))
    split_blocks(1, 0, SPLIT_EARLY)
    p_three(0, 0)
    p_three(0, 1)
    wait(("wout", 0))
    wait(("ssm", 0))
    wait(("conv0", 1))
    wait(("conv", 1))
    p_four(0, 0)
    p_four(0, 1)
    wait(("wout", 1))
    wait(("ssm", 1))

    def step(t, c):
        def chunks(off, stage):
            v = t - off
            l = jnp.where(v >= NEXT, 1, 0)
            i = v - NEXT * l

            @pl.when((v >= 0) & (i < NCH))
            def _():
                stage(l, i)

        def halves(at, stage):
            h = jnp.where(t >= at + HC, 1, 0)

            @pl.when((t == at) | (t == at + HC))
            def _():
                stage(1, h)

        halves(T_FRONT + 1, p_two)
        halves(T_FRONT + P_WAIT, p_three)
        halves(NEXT, p_four)
        chunks(0, stage_a)

        @pl.when((t >= HC) & (t < HC + KB - SPLIT_EARLY))
        def _():
            split_block(1, t - HC + SPLIT_EARLY)

        chunks(OFF_B, stage_b)
        chunks(OFF_C, stage_c)
        chunks(OFF_D, stage_d)
        chunks(OFF_E, stage_e)
        chunks(OFF_F, stage_f)

        def enter(l, h):
            hidden(l, h)
            front(l, h)
            p_one(l, h)

        halves(T_FRONT, enter)
        return c

    lax.fori_loop(0, NEXT + NCH + OFF_F, step, 0)


def write_out(resid, conv, ssm, resid_out, conv_out, ssm_out, sem):
    copies = [(resid, resid_out), (conv, conv_out)]
    for l in range(2):
        for q in range(4):
            part = pl.ds(q * (ROWS // 4), ROWS // 4)
            copies.append((ssm.at[l, part], ssm_out.at[l, part]))
    copies = [pltpu.make_async_copy(s, d, sem.at[i]) for i, (s, d) in enumerate(copies)]
    for c in copies:
        c.start()
    for c in copies:
        c.wait()


def solution(mesh):
    hbm = pl.BlockSpec(memory_space=pl.ANY)
    vmem = pl.BlockSpec(memory_space=pltpu.VMEM)
    V = pltpu.VMEM
    dma = pltpu.SemaphoreType.DMA

    def device_step(residual, norm_w, w_in, conv_w, conv_b, w_x, w_dt, b_dt, a_log, d_skip, w_out, conv_state, ssm_state):
        conv_t = jnp.transpose(conv_state, (0, 2, 1, 3))
        w_xt = jnp.transpose(w_x, (0, 2, 1))
        scratch = [
            V((2, D), BF16), V((2, 4, E), BF16), V((2, E), BF16), V((2, PW, E), BF16), V((2, RANK, E), BF16),
            V((2, E), F32), V((2, N, E), F32), V((2, E), F32),
            V((2, D, 2, E), BF16), V((2, D, E), BF16), V((4, 2 * KD, 128), F32), V((2, E, D), BF16), V((2, ROWS, E), BF16),
            V((ROWS, D), BF16), V((ROWS, E), BF16), V((ROWS, E), F32), V((ROWS, E), F32), V((ROWS, E), F32), V((ROWS, E), F32),
            V((ROWS, 128), F32), V((N, E), F32),
            V((2, PW, HR), F32), V((2, PH, HR), BF16), V((2, 2, PH, HR), BF16), V((2, PH, HR), BF16), V((2, 2, 3, PH, HR), BF16),
            V((2, 2, PW, HR), F32),
            V((NCH, CR, HALF), F32), V((NCH, CR, HALF), BF16), V((2, NCH, CR, HALF), BF16), V((NCH, CR, HALF), BF16),
            V((2, NCH, CR, HALF), BF16), V((NCH, CR, HALF), BF16), V((2, NCH, CR, HALF), BF16), V((2, 2, NCH, CR, HALF), BF16),
            dma((8,)), dma, dma((2, KB)), dma((4,)), dma((2,)), dma((2,)),
            dma((2, 2)), dma((2, 2)), dma((2, 2, 3)), dma((2, 2, 3)), dma((2, 2)), dma((2, 2)),
        ] + [dma((2, NCH))] * 10
        resid, conv_out, ssm = pl.pallas_call(
            body,
            out_shape=(V((ROWS, D), F32), V((2, 3, ROWS, E), BF16), V((2, ROWS, N, E), F32)),
            in_specs=[hbm] * 13,
            out_specs=(vmem, vmem, vmem),
            scratch_shapes=scratch,
            compiler_params=pltpu.CompilerParams(collective_id=0, has_side_effects=True, vmem_limit_bytes=42 * 1024 * 1024),
        )(residual, norm_w, w_in, conv_w, conv_b, w_xt, w_dt, b_dt, a_log, d_skip, w_out, conv_t, ssm_state)
        resid, conv_out, ssm = (pltpu.with_memory_space_constraint(v, V) for v in (resid, conv_out, ssm))
        resid, conv_out, ssm = pl.pallas_call(
            write_out,
            out_shape=[jax.ShapeDtypeStruct(v.shape, v.dtype) for v in (resid, conv_out, ssm)],
            in_specs=[vmem] * 3,
            out_specs=[hbm] * 3,
            scratch_shapes=[dma((10,))],
            compiler_params=pltpu.CompilerParams(vmem_limit_bytes=24 * 1024 * 1024),
        )(resid, conv_out, ssm)
        return resid, jnp.transpose(conv_out, (0, 2, 1, 3)), ssm

    cache_spec = P(None, 'dp', None, 'tp')
    in_specs = (P('dp', None), P(None, None), P(None, None, None, 'tp'), P(None, None, 'tp'), P(None, 'tp'), P(None, 'tp', None), P(None, None, 'tp'), P(None, 'tp'), P(None, None, 'tp'), P(None, 'tp'), P(None, 'tp', None), cache_spec, cache_spec)
    out_specs = (P('dp', None), cache_spec, cache_spec)
    return jax.shard_map(device_step, mesh=mesh, in_specs=in_specs, out_specs=out_specs, check_vma=False)
```

time: 94.6 us -> 85.3 us (0.902)
  local copies, waits for them, and re-layouts: 8.62 us -> 0 us
    unnamed x3 -> x0, local copies, waits for them, and re-layouts: 8.62 us -> none
    pallas_call x1, Pallas kernels: 85.2 us -> 77.3 us  [device_step(): pl.pallas_call(body, out_shape=(V((ROWS, D), F32), V((2, 3, ROWS, E), BF1...]
    pallas_call x0 -> x1, Pallas kernels: none -> 7.09 us  [device_step(): pl.pallas_call(write_out, out_shape=[jax.ShapeDtypeStruct(v.shape, v.dtyp...]
where the time goes in v2:
time: 85.3 us; the launch traced here: 85.1 us
  Pallas kernels  84.4 us (99%)
    pallas_call x1, Pallas kernels, device_step(): pl.pallas_call(body, out_shape=(V((ROWS, D), F32), V((2, 3, ROWS, E), BF1...  77.3 us
    pallas_call x1, Pallas kernels, device_step(): pl.pallas_call(write_out, out_shape=[jax.ShapeDtypeStruct(v.shape, v.dtyp...  7.09 us

profile of v2, /device:TPU:0, one launch (start us, length us, event | category | flops | bytes accessed | tf_op | source)
XLA Modules:
  0.0 85.1 jit_solution(17966573874374034210)
XLA Ops:
  0.6 77.3 %shard_map.148 = (f32[256,2048]{1,0:T(8,128)S(1)}, bf16[2,3,256,512]{3,2,1,0:T(8,128)(2,1)S(1)}, f32[2,256,16,512]{3,2,1,0:T(8,128)S(1)}) custom-call(f32[256,2048]{1,0:T(8,128)} %resid_in.1, bf16[2,2048]{1,0:T(2,128)(2,1)} %norm_w.1, bf16[2,2048,2,512]{3,2,1,0:T(2,128)(2,1)} %w_in.1, bf16[2,4,512]{2,1,0:T(4,128)(2,1)} %conv_w.1, bf16[2,512]{1,0:T(2,128)(2,1)} %conv_b.1, ...), custom_call_target="tpu_custom_call" | custom-call | tf_op jit(solution)/shard_map/pallas_call | solution.py:414
  78.0 7.1 %shard_map.149 = (f32[256,2048]{1,0:T(8,128)}, bf16[2,3,256,512]{3,2,1,0:T(8,128)(2,1)}, f32[2,256,16,512]{3,2,1,0:T(8,128)}) custom-call(f32[256,2048]{1,0:T(8,128)S(1)} %get-tuple-element.9.resid, bf16[2,3,256,512]{3,2,1,0:T(8,128)(2,1)S(1)} %get-tuple-element.10.conv, f32[2,256,16,512]{3,2,1,0:T(8,128)S(1)} %get-tuple-element.11.ssm), custom_call_target="tpu_custom_call" | custom-call | tf_op jit(solution)/shard_map/pallas_call | solution.py:423

commit v3 on v2

v3 whole, which is shorter than its diff:
```python
import functools

import jax
import jax.numpy as jnp
from jax import lax
from jax.experimental import pallas as pl
from jax.experimental.pallas import tpu as pltpu
from jax.sharding import PartitionSpec as P

MESH = pl.DeviceIdType.MESH
LOG2E = 1.4426950408889634
F32, BF16 = jnp.float32, jnp.bfloat16

ROWS = 256
D = 2048
E = 512
N = 16
RANK = 128
PW = RANK + 2 * N
NCH = 8
CR = ROWS // NCH
HALF = D // 2
KB = 8
KD = D // KB
HR = ROWS // 2
HC = NCH // 2
PH = PW // 2
OFF_B, OFF_C, OFF_D, OFF_E, OFF_F, OFF_G = 1, 4, 7, 10, 11, 13
T_FRONT = HC - 1 + OFF_F
P_WAIT = 4
NEXT = T_FRONT + P_WAIT + 1


def silu(v):
    return v * jax.nn.sigmoid(v)


def rms(v, axis, eps):
    return v * lax.rsqrt(jnp.mean(v * v, axis=axis, keepdims=True) + eps)


def body(
    resid_in, norm_w, w_in, conv_w, conv_b, w_xt, w_dt, b_dt, a_log, d_skip, w_out, conv_in, ssm_in,
    resid, conv_out, ssm,
    v_norm, v_convw, v_convb, v_wxt, v_wdt, v_bdt, v_alog, v_dskip,
    w_raw, w_xz, s32, v_wout, conv0,
    hid, xcb, gate, dtb, dtx, dsx, bcb, a2,
    p_own, p_sa, p_ra, p_sb, p_rb, p_full,
    own, o_sa, o_ra, o_sb, o_rb, o_sc, o_rc, tot,
    small_sem, resid_sem, win_sem, conv_sem, ssm_sem, wout_sem,
    pa_send, pa_recv, pb_send, pb_recv, pf_send, pf_recv,
    a_send, a_recv, b_send, b_recv, c_send, c_recv, t_send, t_recv, f_send, f_recv,
):
    dp = lax.axis_index("dp")
    me = lax.axis_index("tp")
    core = lax.rem(me, 2)
    z = me // 2
    is_end = (z == 0) | (z == 3)
    is_mid = (z == 1) | (z == 2)
    partner = me + 1 - 2 * core
    zodd = lax.rem(z, 2)
    zpair = me + 2 - 4 * zodd
    midpeer = (3 - z) * 2 + core

    def dev(t):
        return (dp, t)

    def remote(src, dst, ssem, rsem, target):
        return pltpu.make_async_remote_copy(
            src_ref=src, dst_ref=dst, send_sem=ssem, recv_sem=rsem, device_id=dev(target), device_id_type=MESH)

    barrier = pltpu.get_barrier_semaphore()
    pl.semaphore_signal(barrier, inc=1, device_id=dev(partner), device_id_type=MESH)
    for k in range(1, 4):
        pl.semaphore_signal(barrier, inc=1, device_id=dev(lax.rem(me + 2 * k, 8)), device_id_type=MESH)

    copies = {}

    def load(key, src, dst, sem):
        c = pltpu.make_async_copy(src, dst, sem)
        c.start()
        copies[key] = c

    def wait(key):
        copies.pop(key).wait()

    def load_win(l):
        for kb in range(KB):
            rows = pl.ds(kb * KD, KD)
            for j in range(4):
                pltpu.make_async_copy(w_in.at[l, rows, :, pl.ds(j * 128, 128)], w_raw.at[l, kb, j], win_sem.at[kb]).start()
            copies["win", l, kb] = pltpu.make_async_copy(w_raw.at[l, kb], w_raw.at[l, kb], win_sem.at[kb])

    def load_conv(l):
        load(("conv0", l), conv_in.at[l, 0], conv0.at[l], conv_sem.at[2 * l])
        load(("conv", l), conv_in.at[l, pl.ds(1, 2)], conv_out.at[l, pl.ds(0, 2)], conv_sem.at[2 * l + 1])

    def load_state(l):
        load(("wout", l), w_out.at[l], v_wout.at[l], wout_sem.at[l])
        for n in range(N):
            pltpu.make_async_copy(ssm_in.at[l, :, n, :], ssm.at[l, n], ssm_sem.at[l]).start()
        copies["ssm", l] = pltpu.make_async_copy(ssm.at[l], ssm.at[l], ssm_sem.at[l])

    load("norm", norm_w, v_norm, small_sem.at[0])
    for i in range(NCH):
        load(("resid", i), resid_in.at[pl.ds(i * CR, CR)], resid.at[pl.ds(i * CR, CR)], resid_sem.at[i])
    load_win(0)
    small = ((conv_w, v_convw), (conv_b, v_convb), (w_xt, v_wxt), (w_dt, v_wdt), (b_dt, v_bdt), (a_log, v_alog), (d_skip, v_dskip))
    for i, (s, d) in enumerate(small):
        load(("small", i), s, d, small_sem.at[i + 1])
    load_conv(0)

    late = [("wout", 1), ("conv0", 1), ("conv", 1)] + [("ssm", 1)]

    def row_of(ref, l):
        v = ref[...].astype(F32)
        return jnp.where(l == 0, v[0:1, :], v[1:2, :])

    def unpack(l, kb):
        for j in range(4):
            s32[kb, j] = w_raw[l, kb, j].reshape(2 * KD, 128).astype(F32)

    def pack(kb):
        rows = pl.ds(pl.multiple_of(kb * KD, KD), KD)
        for w in range(2):
            for j in range(4):
                w_xz[w, rows, j * 128:(j + 1) * 128] = s32[kb, j, pl.ds(w, KD, stride=2), :].astype(BF16)

    def normed(l, i):
        rows = pl.ds(pl.multiple_of(i * CR, CR), CR)
        hid[rows, :] = (rms(resid[rows, :], 1, 1e-5) * row_of(v_norm, l)).astype(BF16)

    def hidden(l, h):
        def step(i, c):
            normed(l, h * HC + i)
            return c

        lax.fori_loop(0, HC, step, 0)

    def front(l, h):
        rows = pl.ds(pl.multiple_of(h * HR, HR), HR)
        x_b = jnp.dot(hid[rows, :], w_xz[0], preferred_element_type=F32).astype(BF16)
        conv_out[l, 2, rows, :] = x_b
        gate[rows, :] = silu(jnp.dot(hid[rows, :], w_xz[1], preferred_element_type=F32).astype(BF16).astype(F32))
        cw = v_convw[l].astype(F32)
        pre = row_of(v_convb, l) + cw[3:4, :] * conv_out[l, 2, rows, :].astype(F32)
        pre = pre + cw[0:1, :] * conv0[l, rows, :].astype(F32)
        pre = pre + cw[1:2, :] * conv_out[l, 0, rows, :].astype(F32)
        pre = pre + cw[2:3, :] * conv_out[l, 1, rows, :].astype(F32)
        xcb[rows, :] = silu(pre).astype(BF16)
        dsx[rows, :] = row_of(v_dskip, l) * xcb[rows, :].astype(F32)
        p_own[h] = lax.dot_general(v_wxt[l], xcb[rows, :], (((1,), (1,)), ((), ())), preferred_element_type=F32)

    mine = pl.ds(pl.multiple_of(core * PH, PH), PH)
    theirs = pl.ds(pl.multiple_of((1 - core) * PH, PH), PH)

    def copy_pa(l, h):
        return remote(p_sa.at[l, h], p_ra.at[l, h], pa_send.at[h], pa_recv.at[h], partner)

    def copy_pb(l, h, k):
        return remote(p_sb.at[l, h], p_rb.at[l, h, k - 1], pb_send.at[h, k - 1], pb_recv.at[h, k - 1], lax.rem(me + 2 * k, 8))

    def copy_pf(l, h):
        return remote(p_full.at[l, h, mine], p_full.at[l, h, mine], pf_send.at[h], pf_recv.at[h], partner)

    def p_one(l, h):
        p_sa[l, h] = p_own[h, theirs, :].astype(BF16)
        copy_pa(l, h).start()

    def p_two(l, h):
        copy_pa(l, h).wait_recv()
        p_sb[l, h] = (p_own[h, mine, :] + p_ra[l, h].astype(F32)).astype(BF16)
        for k in range(1, 4):
            copy_pb(l, h, k).start()

    def p_three(l, h):
        for k in range(1, 4):
            copy_pb(l, h, k).wait_recv()
        total = jnp.zeros((PH, HR), F32)
        parts = [p_sb[l, h].astype(F32)] + [p_rb[l, h, k].astype(F32) for k in range(3)]
        for chip in range(4):
            d = lax.rem(z - chip + 4, 4)
            total = total + jnp.where(d == 0, parts[0], jnp.where(d == 1, parts[1], jnp.where(d == 2, parts[2], parts[3])))
        p_full[l, h, mine, :] = total
        copy_pf(l, h).start()

    def p_left(l, h):
        copy_pa(l, h).wait_send()
        for k in range(1, 4):
            copy_pb(l, h, k).wait_send()
        copy_pf(l, h).wait_send()

    def rates(l):
        for n in range(N):
            a2[l, n] = jnp.broadcast_to(-jnp.exp(v_alog[l, n:n + 1, :]) * LOG2E, (8, E))

    def p_four(l, h):
        copy_pf(l, h).wait_recv()
        rows = pl.ds(pl.multiple_of(h * HR, HR), HR)
        pt = p_full[l, h]
        low = rms(pt[:RANK].T, 1, 1e-6).astype(BF16)
        lin = jnp.dot(low, v_wdt[l], preferred_element_type=F32) + row_of(v_bdt, l)
        dt = jnp.maximum(lin, 0.0) + jnp.log1p(jnp.exp(-jnp.abs(lin)))
        dtb[rows, :] = dt
        dtx[rows, :] = dt * xcb[rows, :].astype(F32)
        b = rms(pt[RANK:RANK + N], 0, 1e-6)
        c = rms(pt[RANK + N:], 0, 1e-6)
        bc = jnp.concatenate([b, c, jnp.zeros((128 - 2 * N, HR), F32)], axis=0)
        bcb[rows, :] = bc.T

    def stage_a(l, i):
        r0 = pl.multiple_of(i * CR, CR)

        rows = pl.ds(r0, CR)
        bc = bcb[rows, :]
        dt = dtb[rows, :]
        dx = dtx[rows, :]
        y = dsx[rows, :]
        for n in range(N):
            rate = jnp.concatenate([a2[l, n]] * (CR // 8), axis=0)
            new = jnp.exp2(dt * rate) * ssm[l, n, rows, :] + dx * bc[:, n:n + 1]
            ssm[l, n, rows, :] = new
            y = y + new * bc[:, N + n:N + n + 1]
        yg = (y * gate[rows, :]).astype(BF16)
        their_cols = pl.ds(pl.multiple_of((1 - core) * HALF, HALF), HALF)
        our_cols = pl.ds(pl.multiple_of(core * HALF, HALF), HALF)
        o_sa[i] = jnp.dot(yg, v_wout[l, :, their_cols], preferred_element_type=F32).astype(BF16)
        copy_a(l, i).start()
        own[i] = jnp.dot(yg, v_wout[l, :, our_cols], preferred_element_type=F32)

    def copy_a(l, i):
        return remote(o_sa.at[i], o_ra.at[l, i], a_send.at[i], a_recv.at[i], partner)

    def copy_b(l, i):
        return remote(o_sb.at[i], o_rb.at[l, i], b_send.at[i], b_recv.at[i], zpair)

    def copy_c(l, i):
        return remote(o_sc.at[i], o_rc.at[l, i], c_send.at[i], c_recv.at[i], midpeer)

    def copy_t(l, i):
        return remote(tot.at[l, core, i], tot.at[l, core, i], t_send.at[i], t_recv.at[i], zpair)

    def copy_f(l, i):
        return remote(tot.at[l, core, i], tot.at[l, core, i], f_send.at[i], f_recv.at[i], partner)

    def stage_b(l, i):
        copy_a(l, i).wait_recv()
        chip = own[i] + o_ra[l, i].astype(F32)

        @pl.when(is_end)
        def _():
            o_sb[i] = chip.astype(BF16)
            copy_b(l, i).start()

        @pl.when(is_mid)
        def _():
            own[i] = chip

    def stage_c(l, i):
        @pl.when(is_mid)
        def _():
            copy_b(l, i).wait_recv()
            o_sc[i] = (own[i] + o_rb[l, i].astype(F32)).astype(BF16)
            copy_c(l, i).start()

    def stage_d(l, i):
        @pl.when(is_mid)
        def _():
            copy_c(l, i).wait_recv()
            tot[l, core, i] = (o_sc[i].astype(F32) + o_rc[l, i].astype(F32)).astype(BF16)
            copy_t(l, i).start()
            copy_f(l, i).start()

    def stage_e(l, i):
        @pl.when(is_end)
        def _():
            copy_t(l, i).wait_recv()
            copy_f(l, i).start()

    def stage_f(l, i):
        copy_f(l, i).wait_recv()
        rows = pl.ds(pl.multiple_of(i * CR, CR), CR)
        resid[rows, :HALF] = resid[rows, :HALF] + tot[l, 0, i].astype(F32)
        resid[rows, HALF:] = resid[rows, HALF:] + tot[l, 1, i].astype(F32)

    def stage_g(l, i):
        copy_a(l, i).wait_send()
        copy_f(l, i).wait_send()

        @pl.when(is_end)
        def _():
            copy_b(l, i).wait_send()

        @pl.when(is_mid)
        def _():
            copy_c(l, i).wait_send()
            copy_t(l, i).wait_send()

    wait("norm")
    for i in range(NCH):
        wait(("resid", i))
        normed(0, i)
    for kb in range(KB):
        wait(("win", 0, kb))
        unpack(0, kb)
        if kb > 0:
            pack(kb - 1)
    pack(KB - 1)
    load_win(1)
    load_state(0)
    for i in range(len(small)):
        wait(("small", i))
    wait(("conv0", 0))
    wait(("conv", 0))

    def first(h, c):
        front(0, h)

        @pl.when(h == 0)
        def _():
            pl.semaphore_wait(barrier, 4)

        p_one(0, h)
        return c

    lax.fori_loop(0, 2, first, 0)
    p_two(0, 0)
    rates(0)
    rates(1)
    for kb in range(KB):
        wait(("win", 1, kb))

    def unpack_next(kb, c):
        unpack(1, kb)
        return c

    def pack_next(kb, c):
        pack(kb)
        return c

    lax.fori_loop(0, KB, unpack_next, 0)
    p_two(0, 1)
    lax.fori_loop(0, KB, pack_next, 0)
    p_three(0, 0)
    load_conv(1)
    load_state(1)
    for key in [k for k in copies if k not in late]:
        wait(key)
    p_four(0, 0)

    def arrived():
        for key in late:
            wait(key)

    def step(t, c):
        def chunks(off, stage):
            v = t - off
            l = jnp.where(v >= NEXT, 1, 0)
            i = v - NEXT * l

            @pl.when((v >= 0) & (i < NCH))
            def _():
                stage(l, i)

        def halves(at, stage, first_at=None):
            h = jnp.where(t == at, 0, 1)
            l = jnp.where(t >= at, 1, 0)
            now = (t == at) | (t == at + HC)
            if first_at is not None:
                now = now | (t == first_at)

            @pl.when(now)
            def _():
                stage(l, h)

        def enter(l, h):
            hidden(l, h)
            front(l, h)
            p_one(l, h)

        @pl.when(t == NCH)
        def _():
            arrived()
            for h in range(2):
                p_left(0, h)

        halves(NEXT, p_four, HC)
        chunks(0, stage_a)
        chunks(OFF_B, stage_b)
        chunks(OFF_C, stage_c)
        chunks(OFF_D, stage_d)
        halves(T_FRONT + 1, p_two)
        chunks(OFF_E, stage_e)
        chunks(OFF_F, stage_f)
        halves(T_FRONT, enter)
        halves(T_FRONT + P_WAIT, p_three, 2)
        chunks(OFF_G, stage_g)
        return c

    lax.fori_loop(0, NEXT + NCH + OFF_G, step, 0)
    for h in range(2):
        p_left(1, h)


def write_out(resid, conv, ssm, resid_out, conv_out, ssm_out, sem):
    for l in range(2):
        for n in range(N):
            pltpu.make_async_copy(ssm.at[l, n], ssm_out.at[l, :, n, :], sem.at[0]).start()
    others = [pltpu.make_async_copy(resid, resid_out, sem.at[1]), pltpu.make_async_copy(conv, conv_out, sem.at[2])]
    for c in others:
        c.start()
    for c in others:
        c.wait()
    pltpu.make_async_copy(ssm, ssm, sem.at[0]).wait()


def solution(mesh):
    hbm = pl.BlockSpec(memory_space=pl.ANY)
    vmem = pl.BlockSpec(memory_space=pltpu.VMEM)
    V = pltpu.VMEM
    dma = pltpu.SemaphoreType.DMA

    def device_step(residual, norm_w, w_in, conv_w, conv_b, w_x, w_dt, b_dt, a_log, d_skip, w_out, conv_state, ssm_state):
        conv_t = jnp.transpose(conv_state, (0, 2, 1, 3))
        w_xt = jnp.transpose(w_x, (0, 2, 1))
        scratch = [
            V((2, D), BF16), V((2, 4, E), BF16), V((2, E), BF16), V((2, PW, E), BF16), V((2, RANK, E), BF16),
            V((2, E), F32), V((2, N, E), F32), V((2, E), F32),
            V((2, KB, 4, KD, 2, 128), BF16), V((2, D, E), BF16), V((KB, 4, 2 * KD, 128), F32), V((2, E, D), BF16), V((2, ROWS, E), BF16),
            V((ROWS, D), BF16), V((ROWS, E), BF16), V((ROWS, E), F32), V((ROWS, E), F32), V((ROWS, E), F32), V((ROWS, E), F32),
            V((ROWS, 128), F32), V((2, N, 8, E), F32),
            V((2, PW, HR), F32), V((2, 2, PH, HR), BF16), V((2, 2, PH, HR), BF16), V((2, 2, PH, HR), BF16), V((2, 2, 3, PH, HR), BF16),
            V((2, 2, PW, HR), F32),
            V((NCH, CR, HALF), F32), V((NCH, CR, HALF), BF16), V((2, NCH, CR, HALF), BF16), V((NCH, CR, HALF), BF16),
            V((2, NCH, CR, HALF), BF16), V((NCH, CR, HALF), BF16), V((2, NCH, CR, HALF), BF16), V((2, 2, NCH, CR, HALF), BF16),
            dma((8,)), dma((NCH,)), dma((KB,)), dma((4,)), dma((2,)), dma((2,)),
            dma((2,)), dma((2,)), dma((2, 3)), dma((2, 3)), dma((2,)), dma((2,)),
        ] + [dma((NCH,))] * 10
        resid, conv_out, ssm = pl.pallas_call(
            body,
            out_shape=(V((ROWS, D), F32), V((2, 3, ROWS, E), BF16), V((2, N, ROWS, E), F32)),
            in_specs=[hbm] * 13,
            out_specs=(vmem, vmem, vmem),
            scratch_shapes=scratch,
            compiler_params=pltpu.CompilerParams(collective_id=0, has_side_effects=True, vmem_limit_bytes=43 * 1024 * 1024),
        )(residual, norm_w, w_in, conv_w, conv_b, w_xt, w_dt, b_dt, a_log, d_skip, w_out, conv_t, ssm_state)
        resid, conv_out, ssm = (pltpu.with_memory_space_constraint(v, V) for v in (resid, conv_out, ssm))
        resid, conv_out, ssm = pl.pallas_call(
            write_out,
            out_shape=[jax.ShapeDtypeStruct(v.shape, v.dtype) for v in (resid, conv_out, ssm_state)],
            in_specs=[vmem] * 3,
            out_specs=[hbm] * 3,
            scratch_shapes=[dma((3,))],
            compiler_params=pltpu.CompilerParams(vmem_limit_bytes=24 * 1024 * 1024),
        )(resid, conv_out, ssm)
        return resid, jnp.transpose(conv_out, (0, 2, 1, 3)), ssm

    cache_spec = P(None, 'dp', None, 'tp')
    in_specs = (P('dp', None), P(None, None), P(None, None, None, 'tp'), P(None, None, 'tp'), P(None, 'tp'), P(None, 'tp', None), P(None, None, 'tp'), P(None, 'tp'), P(None, None, 'tp'), P(None, 'tp'), P(None, 'tp', None), cache_spec, cache_spec)
    out_specs = (P('dp', None), cache_spec, cache_spec)
    return jax.shard_map(device_step, mesh=mesh, in_specs=in_specs, out_specs=out_specs, check_vma=False)
```

time: 85.3 us -> 77.4 us (0.907)
  Pallas kernels: 84.4 us -> 76.4 us
    pallas_call x1, Pallas kernels: 77.3 us -> 69.5 us  [device_step(): pl.pallas_call(body, out_shape=(V((ROWS, D), F32), V((2, 3, ROWS, E), BF1...]
where the time goes in v3:
time: 77.4 us; the launch traced here: 77.1 us
  Pallas kernels  76.4 us (99%)
    pallas_call x1, Pallas kernels, device_step(): pl.pallas_call(body, out_shape=(V((ROWS, D), F32), V((2, 3, ROWS, E), BF1...  69.5 us
    pallas_call x1, Pallas kernels, device_step(): pl.pallas_call(write_out, out_shape=[jax.ShapeDtypeStruct(v.shape, v.dtyp...  6.96 us

profile of v3, /device:TPU:0, one launch (start us, length us, event | category | flops | bytes accessed | tf_op | source)
XLA Modules:
  0.0 77.1 jit_solution(1400371315537629230)
XLA Ops:
  0.6 69.5 %shard_map.148 = (f32[256,2048]{1,0:T(8,128)S(1)}, bf16[2,3,256,512]{3,2,1,0:T(8,128)(2,1)S(1)}, f32[2,16,256,512]{3,2,1,0:T(8,128)S(1)}) custom-call(f32[256,2048]{1,0:T(8,128)} %resid_in.1, bf16[2,2048]{1,0:T(2,128)(2,1)} %norm_w.1, bf16[2,2048,2,512]{3,2,1,0:T(2,128)(2,1)} %w_in.1, bf16[2,4,512]{2,1,0:T(4,128)(2,1)} %conv_w.1, bf16[2,512]{1,0:T(2,128)(2,1)} %conv_b.1, ...), custom_call_target="tpu_custom_call" | custom-call | tf_op jit(solution)/shard_map/pallas_call | solution.py:439
  70.1 7.0 %shard_map.149 = (f32[256,2048]{1,0:T(8,128)}, bf16[2,3,256,512]{3,2,1,0:T(8,128)(2,1)}, f32[2,256,16,512]{3,2,1,0:T(8,128)}) custom-call(f32[256,2048]{1,0:T(8,128)S(1)} %get-tuple-element.9.resid, bf16[2,3,256,512]{3,2,1,0:T(8,128)(2,1)S(1)} %get-tuple-element.10.conv, f32[2,16,256,512]{3,2,1,0:T(8,128)S(1)} %get-tuple-element.11.ssm), custom_call_target="tpu_custom_call" | custom-call | tf_op jit(solution)/shard_map/pallas_call | solution.py:448

commit v4 on v3

--- a/solution.py
+++ b/solution.py
@@ -25,7 +25,8 @@
 HR = ROWS // 2
 HC = NCH // 2
 PH = PW // 2
-OFF_B, OFF_C, OFF_D, OFF_E, OFF_F, OFF_G = 1, 4, 7, 10, 11, 13
+FIRST = 3
+OFF_B, OFF_C, OFF_D, OFF_E, OFF_F = 1, 4, 7, 10, 11
 T_FRONT = HC - 1 + OFF_F
 P_WAIT = 4
 NEXT = T_FRONT + P_WAIT + 1
@@ -84,12 +85,10 @@
     def wait(key):
         copies.pop(key).wait()
 
-    def load_win(l):
-        for kb in range(KB):
-            rows = pl.ds(kb * KD, KD)
-            for j in range(4):
-                pltpu.make_async_copy(w_in.at[l, rows, :, pl.ds(j * 128, 128)], w_raw.at[l, kb, j], win_sem.at[kb]).start()
-            copies["win", l, kb] = pltpu.make_async_copy(w_raw.at[l, kb], w_raw.at[l, kb], win_sem.at[kb])
+    def load_win(l, blocks):
+        for kb in blocks:
+            rows = pl.ds(kb * 8 * KD, 8 * KD)
+            load(("win", l, kb), w_in.at[l, rows], w_raw.at[l, rows], win_sem.at[l, kb])
 
     def load_conv(l):
         load(("conv0", l), conv_in.at[l, 0], conv0.at[l], conv_sem.at[2 * l])
@@ -98,44 +97,41 @@
     def load_state(l):
         load(("wout", l), w_out.at[l], v_wout.at[l], wout_sem.at[l])
         for n in range(N):
-            pltpu.make_async_copy(ssm_in.at[l, :, n, :], ssm.at[l, n], ssm_sem.at[l]).start()
-        copies["ssm", l] = pltpu.make_async_copy(ssm.at[l], ssm.at[l], ssm_sem.at[l])
+            load_plane(l, n)
+
+    def load_plane(l, n):
+        pltpu.make_async_copy(ssm_in.at[l, :, n, :], ssm.at[l, n], ssm_sem.at[l]).start()
+
+    def wait_planes(l):
+        pltpu.make_async_copy(ssm.at[l], ssm.at[l], ssm_sem.at[l]).wait()
 
     load("norm", norm_w, v_norm, small_sem.at[0])
-    for i in range(NCH):
-        load(("resid", i), resid_in.at[pl.ds(i * CR, CR)], resid.at[pl.ds(i * CR, CR)], resid_sem.at[i])
-    load_win(0)
+    load_win(0, range(FIRST))
+    for i in range(HC):
+        rows = pl.ds(i * 2 * CR, 2 * CR)
+        load(("resid", i), resid_in.at[rows], resid.at[rows], resid_sem.at[i])
+    load_win(0, range(FIRST, KB))
     small = ((conv_w, v_convw), (conv_b, v_convb), (w_xt, v_wxt), (w_dt, v_wdt), (b_dt, v_bdt), (a_log, v_alog), (d_skip, v_dskip))
     for i, (s, d) in enumerate(small):
         load(("small", i), s, d, small_sem.at[i + 1])
     load_conv(0)
 
-    late = [("wout", 1), ("conv0", 1), ("conv", 1)] + [("ssm", 1)]
-
     def row_of(ref, l):
         v = ref[...].astype(F32)
         return jnp.where(l == 0, v[0:1, :], v[1:2, :])
 
     def unpack(l, kb):
-        for j in range(4):
-            s32[kb, j] = w_raw[l, kb, j].reshape(2 * KD, 128).astype(F32)
+        s32[kb] = w_raw[l, pl.ds(pl.multiple_of(kb * 8 * KD, 8 * KD), 8 * KD), :].astype(F32)
 
     def pack(kb):
         rows = pl.ds(pl.multiple_of(kb * KD, KD), KD)
         for w in range(2):
             for j in range(4):
-                w_xz[w, rows, j * 128:(j + 1) * 128] = s32[kb, j, pl.ds(w, KD, stride=2), :].astype(BF16)
+                w_xz[w, rows, j * 128:(j + 1) * 128] = s32[kb, pl.ds(2 * j + w, KD, stride=8), :].astype(BF16)
 
     def normed(l, i):
         rows = pl.ds(pl.multiple_of(i * CR, CR), CR)
         hid[rows, :] = (rms(resid[rows, :], 1, 1e-5) * row_of(v_norm, l)).astype(BF16)
-
-    def hidden(l, h):
-        def step(i, c):
-            normed(l, h * HC + i)
-            return c
-
-        lax.fori_loop(0, HC, step, 0)
 
     def front(l, h):
         rows = pl.ds(pl.multiple_of(h * HR, HR), HR)
@@ -229,19 +225,19 @@
         own[i] = jnp.dot(yg, v_wout[l, :, our_cols], preferred_element_type=F32)
 
     def copy_a(l, i):
-        return remote(o_sa.at[i], o_ra.at[l, i], a_send.at[i], a_recv.at[i], partner)
+        return remote(o_sa.at[i], o_ra.at[l, i], a_send, a_recv.at[i], partner)
 
     def copy_b(l, i):
-        return remote(o_sb.at[i], o_rb.at[l, i], b_send.at[i], b_recv.at[i], zpair)
+        return remote(o_sb.at[i], o_rb.at[l, i], b_send, b_recv.at[i], zpair)
 
     def copy_c(l, i):
-        return remote(o_sc.at[i], o_rc.at[l, i], c_send.at[i], c_recv.at[i], midpeer)
+        return remote(o_sc.at[i], o_rc.at[l, i], c_send, c_recv.at[i], midpeer)
 
     def copy_t(l, i):
-        return remote(tot.at[l, core, i], tot.at[l, core, i], t_send.at[i], t_recv.at[i], zpair)
+        return remote(tot.at[l, core, i], tot.at[l, core, i], t_send, t_recv.at[i], zpair)
 
     def copy_f(l, i):
-        return remote(tot.at[l, core, i], tot.at[l, core, i], f_send.at[i], f_recv.at[i], partner)
+        return remote(tot.at[l, core, i], tot.at[l, core, i], f_send, f_recv.at[i], partner)
 
     def stage_b(l, i):
         copy_a(l, i).wait_recv()
@@ -283,31 +279,37 @@
         resid[rows, :HALF] = resid[rows, :HALF] + tot[l, 0, i].astype(F32)
         resid[rows, HALF:] = resid[rows, HALF:] + tot[l, 1, i].astype(F32)
 
-    def stage_g(l, i):
-        copy_a(l, i).wait_send()
-        copy_f(l, i).wait_send()
+        @pl.when(l == 0)
+        def _():
+            normed(1, i)
+
+    def o_left(l):
+        remote(o_sa, o_sa, a_send, a_recv.at[0], partner).wait_send()
+        remote(tot.at[l, core], tot.at[l, core], f_send, f_recv.at[0], partner).wait_send()
 
         @pl.when(is_end)
         def _():
-            copy_b(l, i).wait_send()
+            remote(o_sb, o_sb, b_send, b_recv.at[0], zpair).wait_send()
 
         @pl.when(is_mid)
         def _():
-            copy_c(l, i).wait_send()
-            copy_t(l, i).wait_send()
-
-    wait("norm")
-    for i in range(NCH):
-        wait(("resid", i))
-        normed(0, i)
+            remote(o_sc, o_sc, c_send, c_recv.at[0], midpeer).wait_send()
+            remote(tot.at[l, core], tot.at[l, core], t_send, t_recv.at[0], zpair).wait_send()
+
     for kb in range(KB):
+        if kb == FIRST:
+            wait("norm")
+            for i in range(HC):
+                wait(("resid", i))
+                normed(0, 2 * i)
+                normed(0, 2 * i + 1)
+            load_state(0)
+            load_win(1, range(KB))
         wait(("win", 0, kb))
         unpack(0, kb)
         if kb > 0:
             pack(kb - 1)
     pack(KB - 1)
-    load_win(1)
-    load_state(0)
     for i in range(len(small)):
         wait(("small", i))
     wait(("conv0", 0))
@@ -342,15 +344,11 @@
     p_two(0, 1)
     lax.fori_loop(0, KB, pack_next, 0)
     p_three(0, 0)
+    wait(("wout", 0))
+    wait_planes(0)
     load_conv(1)
-    load_state(1)
-    for key in [k for k in copies if k not in late]:
-        wait(key)
+    load(("wout", 1), w_out.at[1], v_wout.at[1], wout_sem.at[1])
     p_four(0, 0)
-
-    def arrived():
-        for key in late:
-            wait(key)
 
     def step(t, c):
         def chunks(off, stage):
@@ -374,15 +372,24 @@
                 stage(l, h)
 
         def enter(l, h):
-            hidden(l, h)
             front(l, h)
             p_one(l, h)
 
-        @pl.when(t == NCH)
-        def _():
-            arrived()
+        @pl.when(t < N)
+        def _():
+            load_plane(1, t)
+
+        @pl.when(t == T_FRONT)
+        def _():
             for h in range(2):
                 p_left(0, h)
+            for key in (("wout", 1), ("conv0", 1), ("conv", 1)):
+                wait(key)
+
+        @pl.when(t == NEXT)
+        def _():
+            wait_planes(1)
+            o_left(0)
 
         halves(NEXT, p_four, HC)
         chunks(0, stage_a)
@@ -394,10 +401,10 @@
         chunks(OFF_F, stage_f)
         halves(T_FRONT, enter)
         halves(T_FRONT + P_WAIT, p_three, 2)
-        chunks(OFF_G, stage_g)
         return c
 
-    lax.fori_loop(0, NEXT + NCH + OFF_G, step, 0)
+    lax.fori_loop(0, NEXT + NCH + OFF_F, step, 0)
+    o_left(1)
     for h in range(2):
         p_left(1, h)
 
@@ -423,19 +430,20 @@
     def device_step(residual, norm_w, w_in, conv_w, conv_b, w_x, w_dt, b_dt, a_log, d_skip, w_out, conv_state, ssm_state):
         conv_t = jnp.transpose(conv_state, (0, 2, 1, 3))
         w_xt = jnp.transpose(w_x, (0, 2, 1))
+        w_rows = jnp.transpose(w_in.reshape(2, D, 2, 4, 128), (0, 1, 3, 2, 4)).reshape(2, 8 * D, 128)
         scratch = [
             V((2, D), BF16), V((2, 4, E), BF16), V((2, E), BF16), V((2, PW, E), BF16), V((2, RANK, E), BF16),
             V((2, E), F32), V((2, N, E), F32), V((2, E), F32),
-            V((2, KB, 4, KD, 2, 128), BF16), V((2, D, E), BF16), V((KB, 4, 2 * KD, 128), F32), V((2, E, D), BF16), V((2, ROWS, E), BF16),
+            V((2, 8 * D, 128), BF16), V((2, D, E), BF16), V((KB, 8 * KD, 128), F32), V((2, E, D), BF16), V((2, ROWS, E), BF16),
             V((ROWS, D), BF16), V((ROWS, E), BF16), V((ROWS, E), F32), V((ROWS, E), F32), V((ROWS, E), F32), V((ROWS, E), F32),
             V((ROWS, 128), F32), V((2, N, 8, E), F32),
             V((2, PW, HR), F32), V((2, 2, PH, HR), BF16), V((2, 2, PH, HR), BF16), V((2, 2, PH, HR), BF16), V((2, 2, 3, PH, HR), BF16),
             V((2, 2, PW, HR), F32),
             V((NCH, CR, HALF), F32), V((NCH, CR, HALF), BF16), V((2, NCH, CR, HALF), BF16), V((NCH, CR, HALF), BF16),
             V((2, NCH, CR, HALF), BF16), V((NCH, CR, HALF), BF16), V((2, NCH, CR, HALF), BF16), V((2, 2, NCH, CR, HALF), BF16),
-            dma((8,)), dma((NCH,)), dma((KB,)), dma((4,)), dma((2,)), dma((2,)),
+            dma((8,)), dma((HC,)), dma((2, KB)), dma((4,)), dma((2,)), dma((2,)),
             dma((2,)), dma((2,)), dma((2, 3)), dma((2, 3)), dma((2,)), dma((2,)),
-        ] + [dma((NCH,))] * 10
+        ] + [dma, dma((NCH,))] * 5
         resid, conv_out, ssm = pl.pallas_call(
             body,
             out_shape=(V((ROWS, D), F32), V((2, 3, ROWS, E), BF16), V((2, N, ROWS, E), F32)),
@@ -443,7 +451,7 @@
             out_specs=(vmem, vmem, vmem),
             scratch_shapes=scratch,
             compiler_params=pltpu.CompilerParams(collective_id=0, has_side_effects=True, vmem_limit_bytes=43 * 1024 * 1024),
-        )(residual, norm_w, w_in, conv_w, conv_b, w_xt, w_dt, b_dt, a_log, d_skip, w_out, conv_t, ssm_state)
+        )(residual, norm_w, w_rows, conv_w, conv_b, w_xt, w_dt, b_dt, a_log, d_skip, w_out, conv_t, ssm_state)
         resid, conv_out, ssm = (pltpu.with_memory_space_constraint(v, V) for v in (resid, conv_out, ssm))
         resid, conv_out, ssm = pl.pallas_call(
             write_out,

time: 77.4 us -> 74.8 us (0.966)
  Pallas kernels: 76.4 us -> 74.1 us
    pallas_call x1, Pallas kernels: 69.5 us -> 67.1 us  [device_step(): pl.pallas_call(body, out_shape=(V((ROWS, D), F32), V((2, 3, ROWS, E), BF1...]
where the time goes in v4:
time: 74.8 us; the launch traced here: 74.7 us
  Pallas kernels  74.1 us (99%)
    pallas_call x1, Pallas kernels, device_step(): pl.pallas_call(body, out_shape=(V((ROWS, D), F32), V((2, 3, ROWS, E), BF1...  67.1 us
    pallas_call x1, Pallas kernels, device_step(): pl.pallas_call(write_out, out_shape=[jax.ShapeDtypeStruct(v.shape, v.dtyp...  6.96 us

profile of v4, /device:TPU:0, one launch (start us, length us, event | category | flops | bytes accessed | tf_op | source)
XLA Modules:
  0.0 74.7 jit_solution(13217346568440039775)
XLA Ops:
  0.6 67.1 %shard_map.148 = (f32[256,2048]{1,0:T(8,128)S(1)}, bf16[2,3,256,512]{3,2,1,0:T(8,128)(2,1)S(1)}, f32[2,16,256,512]{3,2,1,0:T(8,128)S(1)}) custom-call(f32[256,2048]{1,0:T(8,128)} %resid_in.1, bf16[2,2048]{1,0:T(2,128)(2,1)} %norm_w.1, bf16[2,16384,128]{2,1,0:T(8,128)(2,1)} %bitcast.8, bf16[2,4,512]{2,1,0:T(4,128)(2,1)} %conv_w.1, bf16[2,512]{1,0:T(2,128)(2,1)} %conv_b.1, ...), custom_call_target="tpu_custom_call" | custom-call | tf_op jit(solution)/shard_map/pallas_call | solution.py:447
  67.7 7.0 %shard_map.149 = (f32[256,2048]{1,0:T(8,128)}, bf16[2,3,256,512]{3,2,1,0:T(8,128)(2,1)}, f32[2,256,16,512]{3,2,1,0:T(8,128)}) custom-call(f32[256,2048]{1,0:T(8,128)S(1)} %get-tuple-element.9.resid, bf16[2,3,256,512]{3,2,1,0:T(8,128)(2,1)S(1)} %get-tuple-element.10.conv, f32[2,16,256,512]{3,2,1,0:T(8,128)S(1)} %get-tuple-element.11.ssm), custom_call_target="tpu_custom_call" | custom-call | tf_op jit(solution)/shard_map/pallas_call | solution.py:456

commit v5 on v4

--- a/solution.py
+++ b/solution.py
@@ -394,8 +394,8 @@
         halves(NEXT, p_four, HC)
         chunks(0, stage_a)
         chunks(OFF_B, stage_b)
+        chunks(OFF_D, stage_d)
         chunks(OFF_C, stage_c)
-        chunks(OFF_D, stage_d)
         halves(T_FRONT + 1, p_two)
         chunks(OFF_E, stage_e)
         chunks(OFF_F, stage_f)

time: 74.8 us -> 74.9 us (level)
  no operation moved by 1% of the time
where the time goes in v5:
time: 74.9 us; the launch traced here: 74.7 us
  Pallas kernels  74.1 us (99%)
    pallas_call x1, Pallas kernels, device_step(): pl.pallas_call(body, out_shape=(V((ROWS, D), F32), V((2, 3, ROWS, E), BF1...  67.1 us
    pallas_call x1, Pallas kernels, device_step(): pl.pallas_call(write_out, out_shape=[jax.ShapeDtypeStruct(v.shape, v.dtyp...  6.96 us

profile of v5, /device:TPU:0, one launch (start us, length us, event | category | flops | bytes accessed | tf_op | source)
XLA Modules:
  0.0 74.7 jit_solution(13847686332927361459)
XLA Ops:
  0.6 67.1 %shard_map.148 = (f32[256,2048]{1,0:T(8,128)S(1)}, bf16[2,3,256,512]{3,2,1,0:T(8,128)(2,1)S(1)}, f32[2,16,256,512]{3,2,1,0:T(8,128)S(1)}) custom-call(f32[256,2048]{1,0:T(8,128)} %resid_in.1, bf16[2,2048]{1,0:T(2,128)(2,1)} %norm_w.1, bf16[2,16384,128]{2,1,0:T(8,128)(2,1)} %bitcast.8, bf16[2,4,512]{2,1,0:T(4,128)(2,1)} %conv_w.1, bf16[2,512]{1,0:T(2,128)(2,1)} %conv_b.1, ...), custom_call_target="tpu_custom_call" | custom-call | tf_op jit(solution)/shard_map/pallas_call | solution.py:447
  67.8 7.0 %shard_map.149 = (f32[256,2048]{1,0:T(8,128)}, bf16[2,3,256,512]{3,2,1,0:T(8,128)(2,1)}, f32[2,256,16,512]{3,2,1,0:T(8,128)}) custom-call(f32[256,2048]{1,0:T(8,128)S(1)} %get-tuple-element.9.resid, bf16[2,3,256,512]{3,2,1,0:T(8,128)(2,1)S(1)} %get-tuple-element.10.conv, f32[2,16,256,512]{3,2,1,0:T(8,128)S(1)} %get-tuple-element.11.ssm), custom_call_target="tpu_custom_call" | custom-call | tf_op jit(solution)/shard_map/pallas_call | solution.py:456
